TPU v7x, 32 devices: a whole 2x2x4 slice. The times are simulated.
32 devices in a mesh: seq: 8 (over y, x, core), head: 4 (over z).
Axes of the slice: x: 2, y: 2, z: 4, core: 2. Of those that a mesh axis runs over, the one named last changes fastest.
Arguments:
- tokens: bfloat16 [2, 4096, 2048], P(None, 'seq'), may hold values from -6 to 6
- cotangent: bfloat16 [2, 4096, 2048], P(None, 'seq'), may hold values from -6 to 6
- decay_rates: float32 [8], replicated, may hold values from 0 to 1, as said below
- retention_gain: float32 [2048], P('seq'), may hold values from 0.1 to 1.9
- channel_gain: float32 [2048], P('seq'), may hold values from 0.1 to 1.9
- query_weight: float32 [2048, 2048], P('seq', 'head'), may hold values from -0.125 to 0.125
- key_weight: float32 [2048, 2048], P('seq', 'head'), may hold values from -0.125 to 0.125
- value_weight: float32 [2048, 3456], P('seq', 'head'), may hold values from -0.125 to 0.125
- swish_weight: float32 [2048, 3456], P('seq', 'head'), may hold values from -0.125 to 0.125
- output_weight: float32 [3456, 2048], P('head', 'seq'), may hold values from -0.109375 to 0.109375
- gate_weight: float32 [2048, 3456], P('seq', 'head'), may hold values from -0.125 to 0.125
- up_weight: float32 [2048, 3456], P('seq', 'head'), may hold values from -0.125 to 0.125
- down_weight: float32 [3456, 2048], P('head', 'seq'), may hold values from -0.109375 to 0.109375
- query_moment: float32 [2048, 2048], P('seq', 'head'), may hold values from -24 to 24
- key_moment: float32 [2048, 2048], P('seq', 'head'), may hold values from -24 to 24
- value_moment: float32 [2048, 3456], P('seq', 'head'), may hold values from -24 to 24
- swish_moment: float32 [2048, 3456], P('seq', 'head'), may hold values from -24 to 24
- output_moment: float32 [3456, 2048], P('head', 'seq'), may hold values from -24 to 24
- gate_moment: float32 [2048, 3456], P('seq', 'head'), may hold values from -24 to 24
- up_moment: float32 [2048, 3456], P('seq', 'head'), may hold values from -24 to 24
- down_moment: float32 [3456, 2048], P('head', 'seq'), may hold values from -24 to 24
- retention_first: float32 [2048], P('seq'), may hold values from -24 to 24
- retention_second: float32 [2048], P('seq'), may hold values from 1 to 100
- channel_first: float32 [2048], P('seq'), may hold values from -24 to 24
- channel_second: float32 [2048], P('seq'), may hold values from 1 to 100
Outputs:
- block_out: bfloat16 [2, 4096, 2048], P(None, 'seq')
- input_gradient: bfloat16 [2, 4096, 2048], P(None, 'seq')
- retention_gain_gradient: float32 [2048], P('seq')
- channel_gain_gradient: float32 [2048], P('seq')
- query_gradient: float32 [2048, 2048], P('seq', 'head')
- key_gradient: float32 [2048, 2048], P('seq', 'head')
- value_gradient: float32 [2048, 3456], P('seq', 'head')
- swish_gradient: float32 [2048, 3456], P('seq', 'head')
- output_gradient: float32 [3456, 2048], P('head', 'seq')
- gate_gradient: float32 [2048, 3456], P('seq', 'head')
- up_gradient: float32 [2048, 3456], P('seq', 'head')
- down_gradient: float32 [3456, 2048], P('head', 'seq')
- retention_gain_updated: float32 [2048], P('seq')
- channel_gain_updated: float32 [2048], P('seq')
- query_updated: float32 [2048, 2048], P('seq', 'head')
- key_updated: float32 [2048, 2048], P('seq', 'head')
- value_updated: float32 [2048, 3456], P('seq', 'head')
- swish_updated: float32 [2048, 3456], P('seq', 'head')
- output_updated: float32 [3456, 2048], P('head', 'seq')
- gate_updated: float32 [2048, 3456], P('seq', 'head')
- up_updated: float32 [2048, 3456], P('seq', 'head')
- down_updated: float32 [3456, 2048], P('head', 'seq')
- query_moment_updated: float32 [2048, 2048], P('seq', 'head')
- key_moment_updated: float32 [2048, 2048], P('seq', 'head')
- value_moment_updated: float32 [2048, 3456], P('seq', 'head')
- swish_moment_updated: float32 [2048, 3456], P('seq', 'head')
- output_moment_updated: float32 [3456, 2048], P('head', 'seq')
- gate_moment_updated: float32 [2048, 3456], P('seq', 'head')
- up_moment_updated: float32 [2048, 3456], P('seq', 'head')
- down_moment_updated: float32 [3456, 2048], P('head', 'seq')
- retention_first_updated: float32 [2048], P('seq')
- retention_second_updated: float32 [2048], P('seq')
- channel_first_updated: float32 [2048], P('seq')
- channel_second_updated: float32 [2048], P('seq')
Inputs may be any that keep to these rules, and one draw needn't show every extreme that they name: `decay_rates`: positive decay rates.
All inputs are finite; a program needn't handle non-finite values.
Results may differ from a plain program's by a relative error of at most 0.015.
The roundings to bfloat16 on the way count: a program that leaves them out, or rounds other values in their place, can miss the bound.
Values may be sent and summed in bfloat16 or wider, within the bound.
A program may use at most 256 MiB of HBM per device.

v0:
```python
import math

import jax
import jax.numpy as jnp
from jax import lax
from jax.sharding import PartitionSpec as P

D = 2048
HEADS = 8
KEY = 256
VAL = 432
FF = 3456


log_base = math.log(10000.0)
coef_first = 3.4445
coef_second = -4.775
coef_third = 2.0315
muon_rate = 0.02
muon_scale = 0.2
adam_rate = 0.1


def shifted(array, axis, by):
    size = lax.axis_size(axis)
    pairs = [(i, i + by) for i in range(size) if 0 <= i + by < size]
    return lax.ppermute(array, axis, pairs)


def rms_scale(values, scale_gain):
    return (
        values * lax.rsqrt(jnp.mean(values * values, axis=-1, keepdims=True) + 1e-06) * scale_gain
    )


def rotate(values, cosine_table, sine_table):
    column = lax.broadcasted_iota(jnp.int32, values.shape, values.ndim - 1)
    swapped = jnp.where(
        column % 2 == 0, -jnp.roll(values, -1, axis=-1), jnp.roll(values, 1, axis=-1)
    )
    return values * cosine_table + swapped * sine_table


def gate_norm(retained_output, swish_in):
    scaled = retained_output * lax.rsqrt(
        jnp.mean(retained_output * retained_output, axis=-1, keepdims=True) + 1e-05
    )
    return jax.nn.silu(swish_in) * scaled.reshape(swish_in.shape)


def inner_activation(gate_in, up_in):
    return jax.nn.gelu(gate_in, approximate=False) * up_in


def orthogonal(blocks):
    current = blocks.astype(jnp.float32)
    frobenius = jnp.sqrt(jnp.sum(current * current, axis=(1, 2), keepdims=True))
    current = current / (frobenius + 1e-07)
    for newton_step in range(5):
        rounded = current.astype(jnp.bfloat16)
        gram_matrix = jnp.einsum(
            "kdc,kde->kce", rounded, rounded, preferred_element_type=jnp.float32
        )
        gram_low = gram_matrix.astype(jnp.bfloat16)
        polynomial = coef_second * gram_matrix + coef_third * jnp.einsum(
            "kce,kef->kcf", gram_low, gram_low, preferred_element_type=jnp.float32
        )
        current = coef_first * current + jnp.einsum(
            "kdc,kcf->kdf",
            rounded,
            polynomial.astype(jnp.bfloat16),
            preferred_element_type=jnp.float32,
        )
    return current.astype(jnp.bfloat16)


def adam_gain(scale_gain, gradient, first_moment, second_moment):
    first_updated = 0.9 * first_moment + 0.1 * gradient
    second_updated = 0.95 * second_moment + 0.05 * gradient * gradient
    return (
        scale_gain - adam_rate * first_updated / (jnp.sqrt(second_updated) + 1e-08),
        first_updated,
        second_updated,
    )


def heads_total(partial_sum):
    return lax.psum(partial_sum, "head")


def shards(
    tokens,
    cotangent,
    decay_rates,
    retention_gain,
    channel_gain,
    query_weight,
    key_weight,
    value_weight,
    swish_weight,
    output_weight,
    gate_weight,
    up_weight,
    down_weight,
    query_moment,
    key_moment,
    value_moment,
    swish_moment,
    output_moment,
    gate_moment,
    up_moment,
    down_moment,
    retention_first,
    retention_second,
    channel_first,
    channel_second,
):
    bfloat = jnp.bfloat16
    single = jnp.float32
    gathered = (
        lax.all_gather(query_weight.astype(bfloat), "seq", axis=0, tiled=True),
        lax.all_gather(key_weight.astype(bfloat), "seq", axis=0, tiled=True),
        lax.all_gather(value_weight.astype(bfloat), "seq", axis=0, tiled=True),
        lax.all_gather(swish_weight.astype(bfloat), "seq", axis=0, tiled=True),
        lax.all_gather(output_weight.astype(bfloat), "seq", axis=1, tiled=True),
        lax.all_gather(gate_weight.astype(bfloat), "seq", axis=0, tiled=True),
        lax.all_gather(up_weight.astype(bfloat), "seq", axis=0, tiled=True),
        lax.all_gather(down_weight.astype(bfloat), "seq", axis=1, tiled=True),
        lax.all_gather(retention_gain.astype(bfloat), "seq", axis=0, tiled=True),
        lax.all_gather(channel_gain.astype(bfloat), "seq", axis=0, tiled=True),
    )
    (
        query_full,
        key_full,
        value_full,
        swish_full,
        output_full,
        gate_full,
        up_full,
        down_full,
        retention_scale,
        channel_scale,
    ) = gathered
    seq_count, block_length, model_width = tokens.shape
    heads_here = HEADS // lax.axis_size("head")
    seq_devices = lax.axis_size("seq")
    retention_single = retention_scale.astype(single)
    channel_single = channel_scale.astype(single)
    stream = tokens.astype(single)
    normed_one, norm_one_back = jax.vjp(rms_scale, stream, retention_single)
    normed_low = normed_one.astype(bfloat)
    queries = jnp.dot(normed_low, query_full, preferred_element_type=single)
    keys_full = jnp.dot(normed_low, key_full, preferred_element_type=single)
    values_low = jnp.dot(normed_low, value_full, preferred_element_type=single).astype(bfloat)
    swish_in = jnp.dot(normed_low, swish_full, preferred_element_type=single)
    positions = (lax.axis_index("seq") * block_length + jnp.arange(block_length)).astype(single)
    pair_index = (jnp.arange(heads_here * KEY) % KEY // 2).astype(single)
    frequency = jnp.exp(-log_base * pair_index / (KEY // 2 - 1))
    angles = positions[:, None] * frequency[None, :]
    cosine_table = jnp.cos(angles)
    sine_table = jnp.sin(angles)
    key_scale = KEY ** (-0.5)
    query_rot = rotate(queries, cosine_table, sine_table).astype(bfloat)
    key_rot = (rotate(keys_full, cosine_table, sine_table) * key_scale).astype(bfloat)
    query_heads = query_rot.reshape(seq_count, block_length, heads_here, KEY)
    key_heads = key_rot.reshape(seq_count, block_length, heads_here, KEY)
    value_heads = values_low.reshape(seq_count, block_length, heads_here, VAL)
    rates = lax.dynamic_slice(decay_rates, (lax.axis_index("head") * heads_here,), (heads_here,))
    steps_in = jnp.arange(block_length, dtype=single)
    offsets = steps_in[:, None] - steps_in[None, :]
    decay_mask = jnp.where(
        offsets >= 0, jnp.exp(-rates[:, None, None] * jnp.maximum(offsets, 0.0)), 0.0
    )
    query_decay = jnp.exp(-rates[None, :] * (steps_in[:, None] + 1.0))
    key_decay = jnp.exp(-rates[None, :] * (block_length - 1.0 - steps_in[:, None]))
    block_decay = jnp.exp(-rates * block_length).reshape(1, heads_here, 1, 1)
    query_rows_decayed = (query_heads.astype(single) * query_decay[None, :, :, None]).astype(bfloat)
    key_rows_decayed = (key_heads.astype(single) * key_decay[None, :, :, None]).astype(bfloat)
    block_local_state = jnp.einsum(
        "suhk,suhv->shkv", key_rows_decayed, value_heads, preferred_element_type=single
    )

    def forward_round(turn, carry):
        received = shifted(carry[1], "seq", 1)
        return (received, block_decay * received + block_local_state)

    incoming, finished = lax.fori_loop(
        0, seq_devices - 1, forward_round, (jnp.zeros_like(block_local_state), block_local_state)
    )
    incoming_low = incoming.astype(bfloat)
    scores = jnp.einsum("sthk,suhk->shtu", query_heads, key_heads, preferred_element_type=single)
    weights_low = (scores * decay_mask[None]).astype(bfloat)
    retained_output = jnp.einsum(
        "shtu,suhv->sthv", weights_low, value_heads, preferred_element_type=single
    )
    retained_output = retained_output + jnp.einsum(
        "sthk,shkv->sthv", query_rows_decayed, incoming_low, preferred_element_type=single
    )
    gated, gate_back = jax.vjp(gate_norm, retained_output, swish_in)
    gated_low = gated.astype(bfloat)
    output_partial = jnp.dot(gated_low, output_full, preferred_element_type=single)
    mixed = stream + heads_total(output_partial)
    normed_two, norm_two_back = jax.vjp(rms_scale, mixed, channel_single)
    normed_two_low = normed_two.astype(bfloat)
    gate_pre = jnp.dot(normed_two_low, gate_full, preferred_element_type=single)
    up_pre = jnp.dot(normed_two_low, up_full, preferred_element_type=single)
    activated, activation_back = jax.vjp(inner_activation, gate_pre, up_pre)
    activated_low = activated.astype(bfloat)
    down_partial = jnp.dot(activated_low, down_full, preferred_element_type=single)
    block_out = (mixed + heads_total(down_partial)).astype(bfloat)
    upstream = cotangent.astype(single)
    down_local = jnp.einsum("sbf,sbd->fd", activated_low, cotangent, preferred_element_type=single)
    activated_grad = jnp.einsum("sbd,fd->sbf", cotangent, down_full, preferred_element_type=single)
    gate_pre_grad, up_pre_grad = activation_back(activated_grad)
    gate_low_grad = gate_pre_grad.astype(bfloat)
    up_low_grad = up_pre_grad.astype(bfloat)
    gate_local = jnp.einsum(
        "sbd,sbf->df", normed_two_low, gate_low_grad, preferred_element_type=single
    )
    up_local = jnp.einsum("sbd,sbf->df", normed_two_low, up_low_grad, preferred_element_type=single)
    normed_two_partial = jnp.einsum(
        "sbf,df->sbd", gate_low_grad, gate_full, preferred_element_type=single
    ) + jnp.einsum("sbf,df->sbd", up_low_grad, up_full, preferred_element_type=single)
    mixed_part, channel_local = norm_two_back(heads_total(normed_two_partial))
    mixed_grad = upstream + mixed_part
    mixed_low = mixed_grad.astype(bfloat)
    output_local = jnp.einsum("sbv,sbd->vd", gated_low, mixed_low, preferred_element_type=single)
    gated_grad = jnp.einsum("sbd,vd->sbv", mixed_low, output_full, preferred_element_type=single)
    retained_grad, swish_in_grad = gate_back(gated_grad)
    retained_low = retained_grad.astype(bfloat)
    incoming_local = jnp.einsum(
        "sthk,sthv->shkv", query_rows_decayed, retained_low, preferred_element_type=single
    )

    def backward_round(turn, carry):
        received = shifted(carry[1], "seq", -1)
        return (received, block_decay * received + incoming_local)

    outgoing_grad, passed = lax.fori_loop(
        0, seq_devices - 1, backward_round, (jnp.zeros_like(incoming_local), incoming_local)
    )
    outgoing_low = outgoing_grad.astype(bfloat)
    score_grad = (
        jnp.einsum("sthv,suhv->shtu", retained_low, value_heads, preferred_element_type=single)
        * decay_mask[None]
    ).astype(bfloat)
    value_heads_grad = jnp.einsum(
        "shtu,sthv->suhv", weights_low, retained_low, preferred_element_type=single
    )
    value_heads_grad = value_heads_grad + jnp.einsum(
        "suhk,shkv->suhv", key_rows_decayed, outgoing_low, preferred_element_type=single
    )
    query_rot_grad = jnp.einsum(
        "shtu,suhk->sthk", score_grad, key_heads, preferred_element_type=single
    )
    query_rot_grad = (
        query_rot_grad
        + jnp.einsum("sthv,shkv->sthk", retained_low, incoming_low, preferred_element_type=single)
        * query_decay[None, :, :, None]
    )
    key_rot_grad = jnp.einsum(
        "shtu,sthk->suhk", score_grad, query_heads, preferred_element_type=single
    )
    key_rot_grad = (
        key_rot_grad
        + jnp.einsum("suhv,shkv->suhk", value_heads, outgoing_low, preferred_element_type=single)
        * key_decay[None, :, :, None]
    )
    query_low_grad = rotate(
        query_rot_grad.reshape(seq_count, block_length, heads_here * KEY), cosine_table, -sine_table
    ).astype(bfloat)
    key_low_grad = (
        rotate(
            key_rot_grad.reshape(seq_count, block_length, heads_here * KEY),
            cosine_table,
            -sine_table,
        )
        * key_scale
    ).astype(bfloat)
    value_low_grad = value_heads_grad.reshape(seq_count, block_length, heads_here * VAL).astype(
        bfloat
    )
    swish_low_grad = swish_in_grad.astype(bfloat)
    query_local = jnp.einsum(
        "sbd,sbn->dn", normed_low, query_low_grad, preferred_element_type=single
    )
    key_local = jnp.einsum("sbd,sbn->dn", normed_low, key_low_grad, preferred_element_type=single)
    value_local = jnp.einsum(
        "sbd,sbn->dn", normed_low, value_low_grad, preferred_element_type=single
    )
    swish_local = jnp.einsum(
        "sbd,sbn->dn", normed_low, swish_low_grad, preferred_element_type=single
    )
    normed_one_partial = (
        jnp.einsum("sbn,dn->sbd", query_low_grad, query_full, preferred_element_type=single)
        + jnp.einsum("sbn,dn->sbd", key_low_grad, key_full, preferred_element_type=single)
        + jnp.einsum("sbn,dn->sbd", value_low_grad, value_full, preferred_element_type=single)
        + jnp.einsum("sbn,dn->sbd", swish_low_grad, swish_full, preferred_element_type=single)
    )
    stream_part, retention_local = norm_one_back(heads_total(normed_one_partial))
    input_gradient = (mixed_grad + stream_part).astype(bfloat)
    (
        query_sum,
        key_sum,
        value_sum,
        swish_sum,
        output_sum,
        gate_sum,
        up_sum,
        down_sum,
        retention_sum,
        channel_sum,
    ) = (
        lax.psum_scatter(query_local, "seq", scatter_dimension=0, tiled=True),
        lax.psum_scatter(key_local, "seq", scatter_dimension=0, tiled=True),
        lax.psum_scatter(value_local, "seq", scatter_dimension=0, tiled=True),
        lax.psum_scatter(swish_local, "seq", scatter_dimension=0, tiled=True),
        lax.psum_scatter(output_local, "seq", scatter_dimension=1, tiled=True),
        lax.psum_scatter(gate_local, "seq", scatter_dimension=0, tiled=True),
        lax.psum_scatter(up_local, "seq", scatter_dimension=0, tiled=True),
        lax.psum_scatter(down_local, "seq", scatter_dimension=1, tiled=True),
        lax.psum_scatter(retention_local, "seq", scatter_dimension=0, tiled=True),
        lax.psum_scatter(channel_local, "seq", scatter_dimension=0, tiled=True),
    )
    retention_gain_updated, retention_first_updated, retention_second_updated = adam_gain(
        retention_gain, retention_sum, retention_first, retention_second
    )
    channel_gain_updated, channel_first_updated, channel_second_updated = adam_gain(
        channel_gain, channel_sum, channel_first, channel_second
    )
    summed = (query_sum, key_sum, value_sum, swish_sum, output_sum, gate_sum, up_sum, down_sum)
    moments = (
        query_moment,
        key_moment,
        value_moment,
        swish_moment,
        output_moment,
        gate_moment,
        up_moment,
        down_moment,
    )
    moments_updated = [
        0.95 * moment_old + gradient for moment_old, gradient in zip(moments, summed)
    ]
    advances = [
        gradient + 0.95 * moment_new for gradient, moment_new in zip(summed, moments_updated)
    ]
    widths = (KEY, KEY, VAL, VAL, VAL, FF // HEADS, FF // HEADS, FF // HEADS)
    by_rows = (False, False, False, False, True, False, False, True)
    row_count = query_sum.shape[0]
    pieces = []
    for advance, block_width, transposed in zip(advances, widths, by_rows):
        if transposed:
            pieces.append(advance.reshape(heads_here, VAL, row_count).transpose(0, 2, 1))
        else:
            blocks = advance.reshape(row_count, heads_here, block_width).transpose(1, 0, 2)
            pieces.append(jnp.pad(blocks, ((0, 0), (0, 0), (0, VAL - block_width))))
    stacked = jnp.concatenate(pieces, axis=0).astype(bfloat)
    block_count = 8 * heads_here
    if seq_devices >= block_count:
        spacing = seq_devices // block_count
        outgoing = jnp.pad(stacked[:, None], ((0, 0), (0, spacing - 1), (0, 0), (0, 0)))
        outgoing = outgoing.reshape(seq_devices, 1, row_count, VAL)
    else:
        owned_count = block_count // seq_devices
        outgoing = stacked.reshape(owned_count, seq_devices, row_count, VAL).transpose(1, 0, 2, 3)
    received = lax.all_to_all(outgoing, "seq", split_axis=0, concat_axis=0, tiled=True)
    item_count = received.shape[1]
    whole = received.transpose(1, 0, 2, 3).reshape(
        item_count, received.shape[0] * received.shape[2], VAL
    )
    update_low = orthogonal(whole)
    spread = update_low.reshape(item_count, received.shape[0], received.shape[2], VAL).transpose(
        1, 0, 2, 3
    )
    returned = lax.all_to_all(spread, "seq", split_axis=0, concat_axis=0, tiled=True)
    if seq_devices >= block_count:
        updates = returned.reshape(block_count, spacing, row_count, VAL)[:, 0]
    else:
        updates = returned.transpose(1, 0, 2, 3).reshape(block_count, row_count, VAL)
    updates = updates.astype(single) * (muon_rate * muon_scale * math.sqrt(D))
    masters = (
        query_weight,
        key_weight,
        value_weight,
        swish_weight,
        output_weight,
        gate_weight,
        up_weight,
        down_weight,
    )
    updated = []
    for position, (master, block_width, transposed) in enumerate(zip(masters, widths, by_rows)):
        piece = updates[position * heads_here : (position + 1) * heads_here]
        if transposed:
            change = piece.transpose(0, 2, 1).reshape(heads_here * VAL, row_count)
        else:
            change = (
                piece[:, :, :block_width]
                .transpose(1, 0, 2)
                .reshape(row_count, heads_here * block_width)
            )
        updated.append(master - change)
    return (
        block_out,
        input_gradient,
        retention_sum,
        channel_sum,
        query_sum,
        key_sum,
        value_sum,
        swish_sum,
        output_sum,
        gate_sum,
        up_sum,
        down_sum,
        retention_gain_updated,
        channel_gain_updated,
        updated[0],
        updated[1],
        updated[2],
        updated[3],
        updated[4],
        updated[5],
        updated[6],
        updated[7],
        moments_updated[0],
        moments_updated[1],
        moments_updated[2],
        moments_updated[3],
        moments_updated[4],
        moments_updated[5],
        moments_updated[6],
        moments_updated[7],
        retention_first_updated,
        retention_second_updated,
        channel_first_updated,
        channel_second_updated,
    )


def solution(mesh):
    placed = (
        P(None, "seq", None),
        P(None, "seq", None),
        P(),
        P("seq"),
        P("seq"),
        P("seq", "head"),
        P("seq", "head"),
        P("seq", "head"),
        P("seq", "head"),
        P("head", "seq"),
        P("seq", "head"),
        P("seq", "head"),
        P("head", "seq"),
        P("seq", "head"),
        P("seq", "head"),
        P("seq", "head"),
        P("seq", "head"),
        P("head", "seq"),
        P("seq", "head"),
        P("seq", "head"),
        P("head", "seq"),
        P("seq"),
        P("seq"),
        P("seq"),
        P("seq"),
    )
    return jax.shard_map(
        shards,
        mesh=mesh,
        in_specs=placed,
        out_specs=(
            P(None, "seq", None),
            P(None, "seq", None),
            P("seq"),
            P("seq"),
            P("seq", "head"),
            P("seq", "head"),
            P("seq", "head"),
            P("seq", "head"),
            P("head", "seq"),
            P("seq", "head"),
            P("seq", "head"),
            P("head", "seq"),
            P("seq"),
            P("seq"),
            P("seq", "head"),
            P("seq", "head"),
            P("seq", "head"),
            P("seq", "head"),
            P("head", "seq"),
            P("seq", "head"),
            P("seq", "head"),
            P("head", "seq"),
            P("seq", "head"),
            P("seq", "head"),
            P("seq", "head"),
            P("seq", "head"),
            P("head", "seq"),
            P("seq", "head"),
            P("seq", "head"),
            P("head", "seq"),
            P("seq"),
            P("seq"),
            P("seq"),
            P("seq"),
        ),
        check_vma=False,
    )
```

profile of v0, /device:TPU:0, one launch (start us, length us, event | category | flops | bytes accessed | tf_op | source)
XLA Modules:
  0.0 2321.1 jit_solution(10588523225127579951)
XLA Ops:
  20.4 10.5 all-gather
  41.4 5.3 fusion.68
  49.4 22.6 all-gather.15.cloned.1.call-done
  87.8 21.1 all-gather.13.cloned.1.call-done
  108.9 7.2 fusion.91
  123.4 183.5 %while.24 = (s32[]{:T(128)}, f32[2,2,256,432]{2,3,1,0:T(8,128)}, f32[2,2,256,432]{2,3,1,0:T(8,128)}, f32[1,2,1,1]{1,3,2,0:T(1,128)S(1)}, f32[2,2,256,432]{2,3,1,0:T(8,128)S(1)}, /*index=5*/s32[]{:T(128)}) while((s32[]{:T(128)}, f32[2,2,256,432]{2,3,1,0:T(8,128)}, f32[2,2,256,432]{2,3,1,0:T(8,128)}, f32[1,2,1,1]{1,3,2,0:T(1,128)S(1)}, ...), condition=%wide.region_2.3_spmd, body=%wide.region_1.2_spmd.sunk | while | flops 884738 | bytes 19464336 | solution.py:187
  130.9 29.1 %collective-permute-start = (f32[2,2,256,432]{2,3,1,0:T(8,128)}, f32[2,2,256,432]{2,3,1,0:T(8,128)S(1)}, u32[]{:S(2)}, u32[]{:S(2)}) collective-permute-start(f32[2,2,256,432]{2,3,1,0:T(8,128)} %get-tuple-element.280), channel_id=1, source_target_pairs={{0,4},{4,8},{8,12},{12,16},{16,20},{20,24},{24,28},{1,5},{5,9},{9,... | collective-permute-start | bytes 5308424 | tf_op jit(solution)/shard_map/while/body/eval_jaxpr/ppermute | solution.py:27
  165.2 32.9 %collective-permute-start = (f32[2,2,256,432]{2,3,1,0:T(8,128)}, f32[2,2,256,432]{2,3,1,0:T(8,128)S(1)}, u32[]{:S(2)}, u32[]{:S(2)}) collective-permute-start(f32[2,2,256,432]{2,3,1,0:T(8,128)} %get-tuple-element.280), channel_id=1, source_target_pairs={{0,4},{4,8},{8,12},{12,16},{16,20},{20,24},{24,28},{1,5},{5,9},{9,... | collective-permute-start | bytes 5308424 | tf_op jit(solution)/shard_map/while/body/eval_jaxpr/ppermute | solution.py:27
  203.4 20.6 collective-permute-start
  229.3 20.6 collective-permute-start
  255.2 20.6 collective-permute-start
  281.0 20.6 collective-permute-start
  312.8 9.9 fusion.30
  322.7 10.4 fusion.28
  339.4 42.4 %all-gather.1 = bf16[8,1,256]{2,1,0:T(2,128)(2,1)S(1)} all-gather(bf16[1,1,256]{2,1,0:T(2,128)(2,1)S(1)} %reshape.456), channel_id=1, replica_groups=mesh['seq'=8,'head'=4] {'seq'}, dimensions={0}, use_global_device_ids=true | all-gather | bytes 4608 | tf_op jit(solution)/shard_map/all_gather | solution.py:130
  381.8 267.3 %all-reduce.10.cloned.1.call-done = f32[2,512,2048]{2,1,0:T(8,128)} async-done(((f32[2,512,2048]{2,1,0:T(8,128)}), f32[2,512,2048]{2,1,0:T(8,128)}) %all-reduce.10.cloned.1.call-update) | async-done | bytes 8388624 | tf_op jit(solution)/shard_map/psum | solution.py:88
  649.2 5.7 multiply_reduce_fusion.2
  661.0 24.1 %all-gather.21.cloned.1.call-done = bf16[2048,864]{0,1:T(8,128)(2,1)} async-done(((bf16[256,864]{0,1:T(8,128)(2,1)}), bf16[2048,864]{0,1:T(8,128)(2,1)}) %all-gather.21.cloned.1.call-update) | async-done | bytes 3538960 | tf_op jit(solution)/shard_map/all_gather | solution.py:126
  685.1 10.2 fusion.118
  695.3 26.7 %all-gather.25.cloned.1.call-done = bf16[864,2048]{1,0:T(8,128)(2,1)} async-done(((bf16[864,256]{1,0:T(8,128)(2,1)}), bf16[864,2048]{1,0:T(8,128)(2,1)}) %all-gather.25.cloned.1.call-update) | async-done | bytes 3538960 | tf_op jit(solution)/shard_map/all_gather | solution.py:128
  722.0 16.8 multiply_convert_fusion.3
  738.8 20.2 all-gather.23.cloned.1.call-done
  759.0 12.8 add_convert_fusion.3
  776.4 7.2 convolution_add_fusion
  784.1 9.4 convolution_bitcast_fusion.1
  793.5 9.4 convolution_bitcast_fusion
  803.0 9.5 convolution_bitcast_fusion.4
  812.7 261.9 %all-reduce.12.cloned.1.call-done = f32[2,512,2048]{2,1,0:T(8,128)} async-done(((f32[2,512,2048]{2,1,0:T(8,128)}), f32[2,512,2048]{2,1,0:T(8,128)}) %all-reduce.12.cloned.1.call-update) | async-done | bytes 8388624 | tf_op jit(solution)/shard_map/psum | solution.py:88
  1074.6 7.6 multiply_reduce_fusion
  1084.6 6.0 fusion.4
  1090.6 11.9 fusion.119
  1117.2 221.4 %while.25 = (s32[]{:T(128)}, f32[2,2,256,432]{2,3,1,0:T(8,128)}, f32[2,2,256,432]{2,3,1,0:T(8,128)S(1)}, f32[1,2,1,1]{1,3,2,0:T(1,128)S(1)}, f32[2,2,256,432]{2,3,1,0:T(8,128)}, /*index=5*/s32[]{:T(128)}) while((s32[]{:T(128)}, f32[2,2,256,432]{2,3,1,0:T(8,128)}, f32[2,2,256,432]{2,3,1,0:T(8,128)S(1)}, f32[1,2,1,1]{1,3,2,0:T(1,128)S(1)}, ...), condition=%wide.region_11.12_spmd, body=%wide.region_10.11_spmd.sunk | while | flops 884738 | bytes 19464336 | solution.py:239
  1126.6 32.0 %collective-permute-done.1 = f32[2,2,256,432]{2,3,1,0:T(8,128)S(1)} collective-permute-done((f32[2,2,256,432]{2,3,1,0:T(8,128)S(1)}, f32[2,2,256,432]{2,3,1,0:T(8,128)S(1)}, u32[]{:S(2)}, u32[]{:S(2)}) %collective-permute-start.1) | collective-permute-done | bytes 1769504 | tf_op jit(solution)/shard_map/while/body/eval_jaxpr/ppermute | solution.py:27
  1162.4 22.5 collective-permute-done.1
  1188.7 42.1 %collective-permute-done.1 = f32[2,2,256,432]{2,3,1,0:T(8,128)S(1)} collective-permute-done((f32[2,2,256,432]{2,3,1,0:T(8,128)S(1)}, f32[2,2,256,432]{2,3,1,0:T(8,128)S(1)}, u32[]{:S(2)}, u32[]{:S(2)}) %collective-permute-start.1) | collective-permute-done | bytes 1769504 | tf_op jit(solution)/shard_map/while/body/eval_jaxpr/ppermute | solution.py:27
  1234.5 22.7 collective-permute-done.1
  1260.9 41.5 %collective-permute-done.1 = f32[2,2,256,432]{2,3,1,0:T(8,128)S(1)} collective-permute-done((f32[2,2,256,432]{2,3,1,0:T(8,128)S(1)}, f32[2,2,256,432]{2,3,1,0:T(8,128)S(1)}, u32[]{:S(2)}, u32[]{:S(2)}) %collective-permute-start.1) | collective-permute-done | bytes 1769504 | tf_op jit(solution)/shard_map/while/body/eval_jaxpr/ppermute | solution.py:27
  1306.2 29.6 %collective-permute-done.1 = f32[2,2,256,432]{2,3,1,0:T(8,128)S(1)} collective-permute-done((f32[2,2,256,432]{2,3,1,0:T(8,128)S(1)}, f32[2,2,256,432]{2,3,1,0:T(8,128)S(1)}, u32[]{:S(2)}, u32[]{:S(2)}) %collective-permute-start.1) | collective-permute-done | bytes 1769504 | tf_op jit(solution)/shard_map/while/body/eval_jaxpr/ppermute | solution.py:27
  1354.1 6.9 convolution_bitcast_fusion.6
  1367.4 6.1 convolution_bitcast_fusion.3
  1375.0 8.4 convolution_bitcast_fusion.2
  1385.0 9.5 convolution_bitcast_fusion.5
  1394.7 11.3 fusion.17
  1413.1 7.3 fusion.37
  1420.4 10.8 add_add_fusion.2
  1442.6 37.0 %reduce-scatter.11.cloned.1.call-done = f32[256,512]{1,0:T(8,128)} async-done(((f32[2048,512]{1,0:T(8,128)}), f32[256,512]{1,0:T(8,128)}) %reduce-scatter.11.cloned.1.call-update) | async-done | bytes 524304 | tf_op jit(solution)/shard_map/reduce_scatter | solution.py:315
  1484.4 64.5 %reduce-scatter.13.cloned.1.call-done = f32[256,864]{0,1:T(8,128)} async-done(((f32[2048,864]{0,1:T(8,128)}), f32[256,864]{0,1:T(8,128)}) %reduce-scatter.13.cloned.1.call-update) | async-done | bytes 884752 | tf_op jit(solution)/shard_map/reduce_scatter | solution.py:316
  1551.5 66.8 %reduce-scatter.15.cloned.1.call-done = f32[256,864]{0,1:T(8,128)} async-done(((f32[2048,864]{0,1:T(8,128)}), f32[256,864]{0,1:T(8,128)}) %reduce-scatter.15.cloned.1.call-update) | async-done | bytes 884752 | tf_op jit(solution)/shard_map/reduce_scatter | solution.py:317
  1620.8 66.8 %reduce-scatter.17.cloned.1.call-done = f32[864,256]{1,0:T(8,128)} async-done(((f32[864,2048]{1,0:T(8,128)}), f32[864,256]{1,0:T(8,128)}) %reduce-scatter.17.cloned.1.call-update) | async-done | bytes 884752 | tf_op jit(solution)/shard_map/reduce_scatter | solution.py:318
  1697.5 40.7 %all-to-all-done = bf16[8,2,256,432]{2,3,1,0:T(8,128)(2,1)S(1)} async-done(((bf16[8,2,256,432]{2,3,1,0:T(8,128)(2,1)}), bf16[8,2,256,432]{2,3,1,0:T(8,128)(2,1)S(1)}, u32[]{:S(2)}, u32[]{:S(2)}) %all-to-all-start) | async-done | bytes 3538976 | tf_op jit(solution)/shard_map/all_to_all | solution.py:367
  1744.9 9.8 multiply_add_fusion.5
  1754.7 7.2 fusion.86
  1761.9 10.6 multiply_add_fusion.4
  1772.5 7.4 fusion.83
  1779.9 10.8 multiply_add_fusion.3
  1790.7 7.3 fusion.80
  1798.0 10.8 multiply_add_fusion.2
  1808.8 8.2 fusion.77
  1817.0 9.4 add_convert_fusion.1
  1833.0 419.5 %all-reduce.14.cloned.1.call-done = (f32[2,512,2048]{2,1,0:T(8,128)}, f32[2,512,2048]{2,1,0:T(8,128)}) async-done(((f32[2,512,2048]{2,1,0:T(8,128)}, f32[2,512,2048]{2,1,0:T(8,128)}), (f32[2,512,2048]{2,1,0:T(8,128)}, f32[2,512,2048]{2,1,0:T(8,128)})) %all-reduce.14.cloned.1.call-update) | async-done | bytes 16777232 | tf_op jit(solution)/shard_map/psum | solution.py:88
  2252.5 6.0 fusion.3
  2258.5 23.8 %all-reduce.4 = (f32[2048]{0:T(1024)S(1)}, f32[2048]{0:T(1024)S(1)}) all-reduce(f32[2048]{0:T(1024)S(1)} %get-tuple-element.110, f32[2048]{0:T(1024)S(1)} %copy-done.77), channel_id=2, replica_groups=mesh['seq'=8,'head'=4] {'seq'}, use_global_device_ids=true, to_apply=%region_15.16.clone | all-reduce | flops 4096 | bytes 32768
  2283.8 9.4 add_convert_fusion
  2293.1 8.8 fusion.6
  (421 shorter events, 247.8 us)
Async XLA Ops:
  7.2 34.1 %all-gather.17.cloned.1.call-start = ((), (), s32[]{:S(2)}) async-start(), calls=%async_computation.13 | async-start | bytes 2359296 | tf_op jit(solution)/shard_map/all_gather | solution.py:122
  9.3 62.6 %all-gather.15.cloned.1.call-start = ((), (), s32[]{:S(2)}) async-start(), calls=%async_computation.12 | async-start | bytes 2359296 | tf_op jit(solution)/shard_map/all_gather | solution.py:121
  11.3 97.6 %all-gather.13.cloned.1.call-start = ((), (), s32[]{:S(2)}) async-start(), calls=%async_computation.11 | async-start | bytes 3981312 | tf_op jit(solution)/shard_map/all_gather | solution.py:123
  13.3 299.4 %all-gather.11.cloned.1.call-start = ((), (), s32[]{:S(2)}) async-start(), calls=%async_computation.10 | async-start | bytes 3981312 | tf_op jit(solution)/shard_map/all_gather | solution.py:124
  14.2 308.5 %all-gather.19.cloned.1.call-start = ((), (), s32[]{:S(2)}) async-start(), calls=%async_computation.14 | async-start | bytes 3981312 | tf_op jit(solution)/shard_map/all_gather | solution.py:125
  15.1 634.0 %all-reduce.10.cloned.1.call-start = ((), (), s32[]{:S(2)}) async-start(), calls=%async_computation.15 | async-start | bytes 16777216 | tf_op jit(solution)/shard_map/psum | solution.py:88
  15.2 62.6 %copy-start.78 = (s32[512]{0:T(512)}, s32[512]{0:T(512)S(1)}, u32[]{:S(2)}) copy-start(s32[512]{0:T(512)S(1)} %get-tuple-element.210) | copy-start | bytes 6148
  15.2 62.6 %copy-start.80 = (s32[512]{0:T(512)}, s32[512]{0:T(512)S(1)}, u32[]{:S(2)}) copy-start(s32[512]{0:T(512)S(1)} %get-tuple-element.211) | copy-start | bytes 6148
  15.2 62.6 %copy-start.84 = (pred[512]{0:T(512)(128)(4,1)}, pred[512]{0:T(512)(128)(4,1)S(1)}, u32[]{:S(2)}) copy-start(pred[512]{0:T(512)(128)(4,1)S(1)} %fusion.140) | copy-start | bytes 1540
  16.7 19.0 copy-start.94
  19.8 89.1 %copy-start.75 = (f32[2,512]{1,0:T(2,128)}, f32[2,512]{1,0:T(2,128)S(1)}, u32[]{:S(2)}) copy-start(f32[2,512]{1,0:T(2,128)S(1)} %fusion.126) | copy-start | bytes 12292
  30.8 282.0 %copy-start.67 = (f32[8,1,256]{2,1,0:T(1,128)}, f32[8,1,256]{2,1,0:T(1,128)S(1)}, u32[]{:S(2)}) copy-start(f32[8,1,256]{2,1,0:T(1,128)S(1)} %convert_element_type.278) | copy-start | bytes 24580
  35.7 42.2 %copy-start.31 = (f32[512,512]{0,1:T(8,128)}, f32[512,512]{0,1:T(8,128)S(1)}, u32[]{:S(2)}) copy-start(f32[512,512]{0,1:T(8,128)S(1)} %get-tuple-element.200) | copy-start | bytes 3145732
  36.5 79.7 %copy-start.61 = (f32[512,2]{0,1:T(2,128)}, f32[512,2]{0,1:T(2,128)S(1)}, u32[]{:S(2)}) copy-start(f32[512,2]{0,1:T(2,128)S(1)} %get-tuple-element.201) | copy-start | bytes 12292
  36.5 270.5 %copy-start.63 = (f32[512,2]{0,1:T(2,128)}, f32[512,2]{0,1:T(2,128)S(1)}, u32[]{:S(2)}) copy-start(f32[512,2]{0,1:T(2,128)S(1)} %get-tuple-element.202) | copy-start | bytes 12292
  38.1 46.2 %copy-start.12 = (f32[2,512,512]{2,1,0:T(8,128)}, f32[2,512,512]{2,1,0:T(8,128)S(1)}, u32[]{:S(2)}) copy-start(f32[2,512,512]{2,1,0:T(8,128)S(1)} %exponential_select_fusion) | copy-start | bytes 6291460
  87.8 28.4 %copy-start.23 = (bf16[2,512,512]{1,2,0:T(8,128)(2,1)S(1)}, bf16[2,512,512]{1,2,0:T(8,128)(2,1)}, u32[]{:S(2)}) copy-start(bf16[2,512,512]{1,2,0:T(8,128)(2,1)} %copy-done.22) | copy-start | bytes 3145732
  123.4 5.7 collective-permute-start
  130.9 32.5 %collective-permute-start = (f32[2,2,256,432]{2,3,1,0:T(8,128)}, f32[2,2,256,432]{2,3,1,0:T(8,128)S(1)}, u32[]{:S(2)}, u32[]{:S(2)}) collective-permute-start(f32[2,2,256,432]{2,3,1,0:T(8,128)} %get-tuple-element.280), channel_id=1, source_target_pairs={{0,4},{4,8},{8,12},{12,16},{16,20},{20,24},{24,28},{1,5},{5,9},{9,... | collective-permute-start | bytes 5308424 | tf_op jit(solution)/shard_map/while/body/eval_jaxpr/ppermute | solution.py:27
  165.2 36.4 %collective-permute-start = (f32[2,2,256,432]{2,3,1,0:T(8,128)}, f32[2,2,256,432]{2,3,1,0:T(8,128)S(1)}, u32[]{:S(2)}, u32[]{:S(2)}) collective-permute-start(f32[2,2,256,432]{2,3,1,0:T(8,128)} %get-tuple-element.280), channel_id=1, source_target_pairs={{0,4},{4,8},{8,12},{12,16},{16,20},{20,24},{24,28},{1,5},{5,9},{9,... | collective-permute-start | bytes 5308424 | tf_op jit(solution)/shard_map/while/body/eval_jaxpr/ppermute | solution.py:27
  203.4 24.0 %collective-permute-start = (f32[2,2,256,432]{2,3,1,0:T(8,128)}, f32[2,2,256,432]{2,3,1,0:T(8,128)S(1)}, u32[]{:S(2)}, u32[]{:S(2)}) collective-permute-start(f32[2,2,256,432]{2,3,1,0:T(8,128)} %get-tuple-element.280), channel_id=1, source_target_pairs={{0,4},{4,8},{8,12},{12,16},{16,20},{20,24},{24,28},{1,5},{5,9},{9,... | collective-permute-start | bytes 5308424 | tf_op jit(solution)/shard_map/while/body/eval_jaxpr/ppermute | solution.py:27
  229.3 24.0 %collective-permute-start = (f32[2,2,256,432]{2,3,1,0:T(8,128)}, f32[2,2,256,432]{2,3,1,0:T(8,128)S(1)}, u32[]{:S(2)}, u32[]{:S(2)}) collective-permute-start(f32[2,2,256,432]{2,3,1,0:T(8,128)} %get-tuple-element.280), channel_id=1, source_target_pairs={{0,4},{4,8},{8,12},{12,16},{16,20},{20,24},{24,28},{1,5},{5,9},{9,... | collective-permute-start | bytes 5308424 | tf_op jit(solution)/shard_map/while/body/eval_jaxpr/ppermute | solution.py:27
  255.2 24.0 %collective-permute-start = (f32[2,2,256,432]{2,3,1,0:T(8,128)}, f32[2,2,256,432]{2,3,1,0:T(8,128)S(1)}, u32[]{:S(2)}, u32[]{:S(2)}) collective-permute-start(f32[2,2,256,432]{2,3,1,0:T(8,128)} %get-tuple-element.280), channel_id=1, source_target_pairs={{0,4},{4,8},{8,12},{12,16},{16,20},{20,24},{24,28},{1,5},{5,9},{9,... | collective-permute-start | bytes 5308424 | tf_op jit(solution)/shard_map/while/body/eval_jaxpr/ppermute | solution.py:27
  281.0 24.0 %collective-permute-start = (f32[2,2,256,432]{2,3,1,0:T(8,128)}, f32[2,2,256,432]{2,3,1,0:T(8,128)S(1)}, u32[]{:S(2)}, u32[]{:S(2)}) collective-permute-start(f32[2,2,256,432]{2,3,1,0:T(8,128)} %get-tuple-element.280), channel_id=1, source_target_pairs={{0,4},{4,8},{8,12},{12,16},{16,20},{20,24},{24,28},{1,5},{5,9},{9,... | collective-permute-start | bytes 5308424 | tf_op jit(solution)/shard_map/while/body/eval_jaxpr/ppermute | solution.py:27
  333.2 351.9 %all-gather.21.cloned.1.call-start = ((), (), s32[]{:S(2)}) async-start(), calls=%async_computation.16 | async-start | bytes 3981312 | tf_op jit(solution)/shard_map/all_gather | solution.py:126
  335.2 386.8 %all-gather.25.cloned.1.call-start = ((), (), s32[]{:S(2)}) async-start(), calls=%async_computation.18 | async-start | bytes 3981312 | tf_op jit(solution)/shard_map/all_gather | solution.py:128
  337.3 421.7 %all-gather.23.cloned.1.call-start = ((), (), s32[]{:S(2)}) async-start(), calls=%async_computation.17 | async-start | bytes 3981312 | tf_op jit(solution)/shard_map/all_gather | solution.py:127
  339.3 735.3 %all-reduce.12.cloned.1.call-start = ((), (), s32[]{:S(2)}) async-start(), calls=%async_computation.19 | async-start | bytes 16777216 | tf_op jit(solution)/shard_map/psum | solution.py:88
  758.9 12.8 copy-start.97
  783.6 647.7 %reduce-scatter.19.cloned.1.call-start = ((), (), s32[]{:S(2)}) async-start(), calls=%async_computation.25 | async-start | bytes 7962624 | tf_op jit(solution)/shard_map/reduce_scatter | solution.py:319
  793.5 641.3 %reduce-scatter.21.cloned.1.call-start = ((), (), s32[]{:S(2)}) async-start(), calls=%async_computation.26 | async-start | bytes 7962624 | tf_op jit(solution)/shard_map/reduce_scatter | solution.py:320
  802.9 634.4 %reduce-scatter.23.cloned.1.call-start = ((), (), s32[]{:S(2)}) async-start(), calls=%async_computation.27 | async-start | bytes 7962624 | tf_op jit(solution)/shard_map/reduce_scatter | solution.py:321
  812.5 627.3 %reduce-scatter.9.cloned.1.call-start = ((), (), s32[]{:S(2)}) async-start(), calls=%async_computation.20 | async-start | bytes 4718592 | tf_op jit(solution)/shard_map/reduce_scatter | solution.py:314
  1074.6 8.2 copy-start.18
  1074.6 10.0 copy-start.36
  1090.6 12.0 copy-start.19
  1090.6 12.0 copy-start.11
  1117.2 221.4 %copy-start.62 = (f32[512,2]{0,1:T(2,128)S(1)}, f32[512,2]{0,1:T(2,128)}, u32[]{:S(2)}) copy-start(f32[512,2]{0,1:T(2,128)} %copy-done.61) | copy-start | bytes 12292
  1117.2 5.7 collective-permute-start.1
  1125.3 33.3 %collective-permute-start.1 = (f32[2,2,256,432]{2,3,1,0:T(8,128)S(1)}, f32[2,2,256,432]{2,3,1,0:T(8,128)S(1)}, u32[]{:S(2)}, u32[]{:S(2)}) collective-permute-start(f32[2,2,256,432]{2,3,1,0:T(8,128)S(1)} %get-tuple-element.298), channel_id=1, source_target_pairs={{4,0},{8,4},{12,8},{16,12},{20,16},{24,20},{28,24},{5,1},{9,5},{13... | collective-permute-start | bytes 5308424 | tf_op jit(solution)/shard_map/while/body/eval_jaxpr/ppermute | solution.py:27
  1161.1 23.8 %collective-permute-start.1 = (f32[2,2,256,432]{2,3,1,0:T(8,128)S(1)}, f32[2,2,256,432]{2,3,1,0:T(8,128)S(1)}, u32[]{:S(2)}, u32[]{:S(2)}) collective-permute-start(f32[2,2,256,432]{2,3,1,0:T(8,128)S(1)} %get-tuple-element.298), channel_id=1, source_target_pairs={{4,0},{8,4},{12,8},{16,12},{20,16},{24,20},{28,24},{5,1},{9,5},{13... | collective-permute-start | bytes 5308424 | tf_op jit(solution)/shard_map/while/body/eval_jaxpr/ppermute | solution.py:27
  1187.4 43.4 %collective-permute-start.1 = (f32[2,2,256,432]{2,3,1,0:T(8,128)S(1)}, f32[2,2,256,432]{2,3,1,0:T(8,128)S(1)}, u32[]{:S(2)}, u32[]{:S(2)}) collective-permute-start(f32[2,2,256,432]{2,3,1,0:T(8,128)S(1)} %get-tuple-element.298), channel_id=1, source_target_pairs={{4,0},{8,4},{12,8},{16,12},{20,16},{24,20},{28,24},{5,1},{9,5},{13... | collective-permute-start | bytes 5308424 | tf_op jit(solution)/shard_map/while/body/eval_jaxpr/ppermute | solution.py:27
  1233.2 24.0 %collective-permute-start.1 = (f32[2,2,256,432]{2,3,1,0:T(8,128)S(1)}, f32[2,2,256,432]{2,3,1,0:T(8,128)S(1)}, u32[]{:S(2)}, u32[]{:S(2)}) collective-permute-start(f32[2,2,256,432]{2,3,1,0:T(8,128)S(1)} %get-tuple-element.298), channel_id=1, source_target_pairs={{4,0},{8,4},{12,8},{16,12},{20,16},{24,20},{28,24},{5,1},{9,5},{13... | collective-permute-start | bytes 5308424 | tf_op jit(solution)/shard_map/while/body/eval_jaxpr/ppermute | solution.py:27
  1259.6 42.8 %collective-permute-start.1 = (f32[2,2,256,432]{2,3,1,0:T(8,128)S(1)}, f32[2,2,256,432]{2,3,1,0:T(8,128)S(1)}, u32[]{:S(2)}, u32[]{:S(2)}) collective-permute-start(f32[2,2,256,432]{2,3,1,0:T(8,128)S(1)} %get-tuple-element.298), channel_id=1, source_target_pairs={{4,0},{8,4},{12,8},{16,12},{20,16},{24,20},{28,24},{5,1},{9,5},{13... | collective-permute-start | bytes 5308424 | tf_op jit(solution)/shard_map/while/body/eval_jaxpr/ppermute | solution.py:27
  1304.9 30.9 %collective-permute-start.1 = (f32[2,2,256,432]{2,3,1,0:T(8,128)S(1)}, f32[2,2,256,432]{2,3,1,0:T(8,128)S(1)}, u32[]{:S(2)}, u32[]{:S(2)}) collective-permute-start(f32[2,2,256,432]{2,3,1,0:T(8,128)S(1)} %get-tuple-element.298), channel_id=1, source_target_pairs={{4,0},{8,4},{12,8},{16,12},{20,16},{24,20},{28,24},{5,1},{9,5},{13... | collective-permute-start | bytes 5308424 | tf_op jit(solution)/shard_map/while/body/eval_jaxpr/ppermute | solution.py:27
  1354.0 125.6 %reduce-scatter.11.cloned.1.call-start = ((), (), s32[]{:S(2)}) async-start(), calls=%async_computation.21 | async-start | bytes 4718592 | tf_op jit(solution)/shard_map/reduce_scatter | solution.py:315
  1361.0 187.9 %reduce-scatter.13.cloned.1.call-start = ((), (), s32[]{:S(2)}) async-start(), calls=%async_computation.22 | async-start | bytes 7962624 | tf_op jit(solution)/shard_map/reduce_scatter | solution.py:316
  1373.5 244.7 %reduce-scatter.15.cloned.1.call-start = ((), (), s32[]{:S(2)}) async-start(), calls=%async_computation.23 | async-start | bytes 7962624 | tf_op jit(solution)/shard_map/reduce_scatter | solution.py:317
  1383.4 304.2 %reduce-scatter.17.cloned.1.call-start = ((), (), s32[]{:S(2)}) async-start(), calls=%async_computation.24 | async-start | bytes 7962624 | tf_op jit(solution)/shard_map/reduce_scatter | solution.py:318
  1394.6 11.3 copy-start.55
  1394.6 857.9 %all-reduce.14.cloned.1.call-start = ((), (), s32[]{:S(2)}) async-start(), calls=%async_computation.28 | async-start | bytes 33554432 | tf_op jit(solution)/shard_map/psum | solution.py:88
  1394.7 11.3 copy-start.99
  1413.1 7.3 copy-start.38
  1434.8 44.9 %copy-start.60 = (f32[256,512]{1,0:T(8,128)S(1)}, f32[256,512]{1,0:T(8,128)}, u32[]{:S(2)}) copy-start(f32[256,512]{1,0:T(8,128)} %param.43) | copy-start | bytes 1572868
  1692.4 45.8 %all-to-all-start = ((bf16[8,2,256,432]{2,3,1,0:T(8,128)(2,1)}), bf16[8,2,256,432]{2,3,1,0:T(8,128)(2,1)S(1)}, u32[]{:S(2)}, u32[]{:S(2)}) async-start(bf16[8,2,256,432]{2,3,1,0:T(8,128)(2,1)} %copy.186), calls=%async_computation.8 | async-start | bytes 7077888 | tf_op jit(solution)/shard_map/all_to_all | solution.py:367
  1828.5 473.5 %all-to-all-start.1 = ((bf16[8,2,256,432]{2,3,1,0:T(8,128)(2,1)}), bf16[8,2,256,432]{2,3,1,0:T(8,128)(2,1)}, u32[]{:S(2)}, u32[]{:S(2)}) async-start(bf16[8,2,256,432]{2,3,1,0:T(8,128)(2,1)} %bitcast.226), calls=%async_computation.9 | async-start | bytes 7077888 | tf_op jit(solution)/shard_map/all_to_all | solution.py:376
  2252.5 29.9 %copy-start.87 = (f32[256]{0:T(256)S(1)}, f32[256]{0:T(256)}, u32[]{:S(2)}) copy-start(f32[256]{0:T(256)} %param.33) | copy-start | bytes 3076
  2252.5 29.9 %copy-start.88 = (f32[256]{0:T(256)S(1)}, f32[256]{0:T(256)}, u32[]{:S(2)}) copy-start(f32[256]{0:T(256)} %param.52) | copy-start | bytes 3076
  2252.5 29.9 %copy-start.89 = (f32[256]{0:T(256)S(1)}, f32[256]{0:T(256)}, u32[]{:S(2)}) copy-start(f32[256]{0:T(256)} %param.53) | copy-start | bytes 3076
  2252.5 30.6 %copy-start.91 = (f32[256]{0:T(256)S(1)}, f32[256]{0:T(256)}, u32[]{:S(2)}) copy-start(f32[256]{0:T(256)} %param.32) | copy-start | bytes 3076
  2252.5 30.6 %copy-start.92 = (f32[256]{0:T(256)S(1)}, f32[256]{0:T(256)}, u32[]{:S(2)}) copy-start(f32[256]{0:T(256)} %param.50) | copy-start | bytes 3076
  2252.5 30.5 %copy-start.93 = (f32[256]{0:T(256)S(1)}, f32[256]{0:T(256)}, u32[]{:S(2)}) copy-start(f32[256]{0:T(256)} %param.51) | copy-start | bytes 3076
  2252.5 31.2 %copy-start.74 = (f32[2,512]{1,0:T(2,128)S(1)}, f32[2,512]{1,0:T(2,128)}, u32[]{:S(2)}) copy-start(f32[2,512]{1,0:T(2,128)} %copy-done.73) | copy-start | bytes 12292
  2283.7 9.4 copy-start.9
  (89 other events, 252.6 us)
Sparse Core Ops, SparseCore 0:
  10.5 30.8 all-gather.16
  43.8 28.0 all-gather.14
  74.4 34.4 all-gather.12
  111.2 38.6 all-gather.10
  152.2 41.3 all-gather.18
  333.3 315.8 all-reduce.9
  651.6 33.4 all-gather.20
  687.5 34.4 all-gather.24
  724.5 34.4 all-gather.22
  783.7 290.8 all-reduce.11
  1078.7 70.9 reduce-scatter.18
  1153.6 78.1 reduce-scatter.20
  1235.9 78.5 reduce-scatter.22
  1354.2 70.4 reduce-scatter.8
  1428.4 51.1 reduce-scatter.10
  1483.6 65.3 reduce-scatter.12
  1552.9 65.3 reduce-scatter.14
  1622.2 65.3 reduce-scatter.16
  1690.2 562.2 all-reduce.13
where the time goes:
time: 2330 us; the launch traced here: 2320 us
  waiting for transfers between devices  1560 us (67%)
  matrix products  308 us (13%)
  starting transfers between devices  166 us (7%)
  other arithmetic  140 us (6%)
  blocking collectives  76.7 us (3%)
  local copies, waits for them, and re-layouts  52.6 us (2%)
    psum x3, waiting for transfers between devices, heads_total(): return lax.psum(partial_sum, 'head')  949 us
    ppermute x14, waiting for transfers between devices, shifted(): return lax.ppermute(array, axis, pairs)  218 us
    ppermute x14, starting transfers between devices, shifted(): return lax.ppermute(array, axis, pairs)  156 us
    reduce_scatter x1, waiting for transfers between devices, shards(): lax.psum_scatter(swish_local, 'seq', scatter_dimension=0, tiled=True)  66.8 us
    reduce_scatter x1, waiting for transfers between devices, shards(): lax.psum_scatter(output_local, 'seq', scatter_dimension=1, tiled=True)  66.8 us
    reduce_scatter x1, waiting for transfers between devices, shards(): lax.psum_scatter(value_local, 'seq', scatter_dimension=0, tiled=True)  64.5 us
    dot_general x5, matrix products, orthogonal(): jnp.einsum('kdc,kcf->kdf', rounded, polynomial.astype(jnp.bfloat16), pref...  51.4 us
  transfers between devices with their start and end apart: 35, of which 28 were waited for; matrix products, arithmetic and copies ran while one was open for 18% of the time, Pallas kernels for 0%

commit v1 on v0

v1 whole, which is shorter than its diff:
```python
import functools
import math

import jax
import jax.numpy as jnp
from jax import lax
from jax.experimental import pallas as pl
from jax.experimental.pallas import tpu as pltpu
from jax.sharding import PartitionSpec as P

D = 2048
HEADS = 8
KEY = 256
VAL = 432
FF = 3456
FBLK = FF // HEADS
SEQS = 2

log_base = math.log(10000.0)
coef_first = 3.4445
coef_second = -4.775
coef_third = 2.0315
muon_rate = 0.02
muon_scale = 0.2
adam_rate = 0.1
bfloat = jnp.bfloat16
single = jnp.float32
MESH = pl.DeviceIdType.MESH
VMEM_ALL = 67043328


def mm(left, right, contract):
    return lax.dot_general(left, right, (contract, ((), ())), preferred_element_type=single)


def nn(left, right):
    return mm(left, right, ((1,), (0,)))


def nt(left, right):
    return mm(left, right, ((1,), (1,)))


def tn(left, right):
    return mm(left, right, ((0,), (0,)))


def core_groups():
    count = lax.axis_size("seq")
    return [list(range(start, count, 2)) for start in (0, 1)]


def sibling(array):
    count = lax.axis_size("seq")
    return lax.ppermute(array, "seq", [(i, i ^ 1) for i in range(count)])


def is_second():
    return lax.axis_index("seq") % 2 == 1


def chips_gathered(stacked):
    return lax.all_gather(stacked, "seq", axis=0, axis_index_groups=core_groups())


def gathered(stacked):
    own = chips_gathered(stacked)
    other = sibling(own)
    second = is_second()
    low = jnp.where(second, other, own)
    high = jnp.where(second, own, other)
    chips, kinds, rows, columns = own.shape
    return [
        jnp.stack([low[:, i], high[:, i]], axis=1).reshape(chips * 2 * rows, columns)
        for i in range(kinds)
    ]


def scattered(locals_):
    count = lax.axis_size("seq")
    second = is_second()
    own, other = [], []
    for array in locals_:
        parts = array.reshape(count // 2, 2, array.shape[0] // count, array.shape[1])
        own.append(jnp.where(second, parts[:, 1], parts[:, 0]))
        other.append(jnp.where(second, parts[:, 0], parts[:, 1]).astype(bfloat))
    received = sibling(jnp.stack(other, axis=1)).astype(single)
    pair = (jnp.stack(own, axis=1) + received).astype(bfloat)
    return lax.psum_scatter(
        pair, "seq", scatter_dimension=0, tiled=False, axis_index_groups=core_groups()
    ).astype(single)


def heads_total(partial_sum):
    return lax.psum(partial_sum.astype(bfloat), "head").astype(single)


def gain_total(local):
    count = lax.axis_size("seq")
    pieces = lax.all_to_all(local.reshape(count, -1), "seq", 0, 0, tiled=True)
    return lax.psum(jnp.sum(pieces, axis=0), "head")


def state_exchange(local, decay, reverse):
    count = lax.axis_size("seq")
    blocks, keys, vals = local.shape
    pieces = local.astype(bfloat).reshape(blocks, count, keys // count, vals)
    pieces = lax.all_to_all(pieces.transpose(1, 0, 2, 3), "seq", 0, 0, tiled=True)
    pieces = pieces.astype(single)
    running = jnp.zeros_like(pieces[0])
    states = [None] * count
    for step in range(count):
        position = count - 1 - step if reverse else step
        states[position] = running.astype(bfloat)
        running = decay * running + pieces[position]
    returned = lax.all_to_all(jnp.stack(states), "seq", 0, 0, tiled=True)
    return returned.transpose(1, 0, 2, 3).reshape(blocks, keys, vals)


def adam_gain(scale_gain, gradient, first_moment, second_moment):
    first_updated = 0.9 * first_moment + 0.1 * gradient
    second_updated = 0.95 * second_moment + 0.05 * gradient * gradient
    return (
        scale_gain - adam_rate * first_updated / (jnp.sqrt(second_updated) + 1e-08),
        first_updated,
        second_updated,
    )


def muon_group(gradients, moments, masters, widths, by_rows, shift):
    heads_here = HEADS // lax.axis_size("head")
    count = lax.axis_size("seq")
    row_count = gradients[0].shape[0]
    moments_updated, pieces, shown = [], [], []
    for gradient, moment, width, transposed in zip(gradients, moments, widths, by_rows):
        if transposed:
            shown.append(gradient.T)
        else:
            shown.append(gradient)
        new = 0.95 * moment + shown[-1]
        moments_updated.append(new)
        advance = shown[-1] + 0.95 * new
        if transposed:
            advance = advance.T
        blocks = advance.astype(bfloat).reshape(row_count, heads_here, width).transpose(1, 0, 2)
        pieces.append(jnp.pad(blocks, ((0, 0), (0, 0), (0, VAL - width))))
    outgoing = jnp.concatenate(pieces, axis=0)
    block_count = outgoing.shape[0]
    if count >= block_count:
        spacing = count // block_count
        place = shift % spacing
        outgoing = jnp.pad(
            outgoing[:, None], ((0, 0), (place, spacing - 1 - place), (0, 0), (0, 0))
        ).reshape(count, 1, row_count, VAL)
    else:
        owned = block_count // count
        outgoing = outgoing.reshape(owned, count, row_count, VAL).transpose(1, 0, 2, 3)
    received = lax.all_to_all(outgoing, "seq", split_axis=0, concat_axis=0, tiled=True)
    items = received.shape[1]
    results = [orthogonal(received[:, i].reshape(count * row_count, VAL)) for i in range(items)]
    spread = jnp.stack([r.reshape(count, row_count, VAL) for r in results], axis=1)
    returned = lax.all_to_all(spread, "seq", split_axis=0, concat_axis=0, tiled=True)
    if count >= block_count:
        updates = returned.reshape(block_count, spacing, row_count, VAL)[:, place]
    else:
        updates = returned.transpose(1, 0, 2, 3).reshape(block_count, row_count, VAL)
    updates = updates.astype(single) * (muon_rate * muon_scale * math.sqrt(D))
    updated = []
    for position, (master, width, transposed) in enumerate(zip(masters, widths, by_rows)):
        piece = updates[position * heads_here : (position + 1) * heads_here, :, :width]
        if transposed:
            change = piece.transpose(0, 2, 1).reshape(heads_here * width, row_count)
        else:
            change = piece.transpose(1, 0, 2).reshape(row_count, heads_here * width)
        updated.append(master - change)
    return shown, moments_updated, updated


def dot(left, right, contract):
    return lax.dot_general(left, right, (contract, ((), ())), preferred_element_type=single)

class Line:
    def __init__(self, upward, rows, half, part, land, sems):
        self.n = lax.axis_size("head")
        self.upward, self.rows, self.half = upward, rows, half
        self.part, self.land = part, land
        self.red_send, self.red_recv, self.cast_send, self.cast_recv = sems
        self.z = lax.axis_index("head")
        self.count = half // rows
    def near(self, flow):
        toward_top = (flow + self.upward) % 2
        return jnp.where(toward_top == 1, self.z, self.n - 1 - self.z)
    def ahead(self, flow):
        toward_top = (flow + self.upward) % 2
        return self.z + 2 * toward_top - 1
    def at(self, flow, c):
        return pl.ds(pl.multiple_of(flow * self.half + c * self.rows, self.rows), self.rows)
    def move(self, flow, c):
        return pltpu.make_async_remote_copy(
            src_ref=self.part.at[self.at(flow, c)], dst_ref=self.land.at[self.at(flow, c)],
            send_sem=self.red_send.at[flow, c], recv_sem=self.red_recv.at[flow, c],
            device_id={"head": self.ahead(flow)}, device_id_type=MESH)
    def back(self, flow, c):
        return pltpu.make_async_remote_copy(
            src_ref=self.land.at[self.at(flow, c)], dst_ref=self.land.at[self.at(flow, c)],
            send_sem=self.cast_send.at[flow, c], recv_sem=self.cast_recv.at[flow, c],
            device_id={"head": 2 * self.z - self.ahead(flow)}, device_id_type=MESH)
    def reduce(self, flow, c):
        near = self.near(flow)
        at = self.at(flow, c)
        @pl.when(near > 0)
        def _():
            self.move(flow, c).wait_recv()
            summed = (self.land[at, :].astype(single) + self.part[at, :].astype(single)).astype(bfloat)
            @pl.when(near == self.n - 1)
            def _():
                self.land[at, :] = summed
            @pl.when(near < self.n - 1)
            def _():
                self.part[at, :] = summed
        @pl.when(near < self.n - 1)
        def _(): self.move(flow, c).start()
        @pl.when(near == self.n - 1)
        def _(): self.back(flow, c).start()
    def cast(self, flow, c):
        near = self.near(flow)
        @pl.when(near < self.n - 1)
        def _():
            self.back(flow, c).wait_recv()
            @pl.when(near > 0)
            def _(): self.back(flow, c).start()
    def finish(self):
        def each(index, carry):
            flow, c = index // self.count, index % self.count
            near = self.near(flow)
            @pl.when(near < self.n - 1)
            def _(): self.move(flow, c).wait_send()
            @pl.when(near > 0)
            def _(): self.back(flow, c).wait_send()
            return carry
        lax.fori_loop(0, 2 * self.count, each, 0)

def enter():
    barrier = pltpu.get_barrier_semaphore()
    z, n = lax.axis_index("head"), lax.axis_size("head")
    @pl.when(z > 0)
    def _(): pl.semaphore_signal(barrier, inc=1, device_id={"head": z - 1}, device_id_type=MESH)
    @pl.when(z < n - 1)
    def _(): pl.semaphore_signal(barrier, inc=1, device_id={"head": z + 1}, device_id_type=MESH)
    pl.semaphore_wait(barrier, jnp.where((z > 0) & (z < n - 1), 2, 1))

def middle_kernel(rows, y_hbm, x_hbm, g_hbm, own_hbm, other_hbm, gain_ref,
                  total_hbm, n2_hbm, m_hbm, da_hbm, db_hbm, pd_hbm, dh_hbm, dy_hbm, gsum_ref,
                  y, x, g, wo, wg, wu, wd, part1, land1, part3, land3,
                  n2s, ms, das, dbs, pds, dhs, dys, in_sems, weight_sems, out_sems, *sems):
    full, width = x.shape
    half = full // 2
    big = 2 * rows
    one = Line(0, rows, half, part1, land1, sems[:4])
    two = Line(1, rows, half, part3, land3, sems[4:])
    count = half // rows
    n = one.n
    loads = [pltpu.make_async_copy(a, b, in_sems.at[i])
             for i, (a, b) in enumerate(((y_hbm, y), (x_hbm, x), (g_hbm, g)))]
    core = lax.axis_index("seq") % 2
    chips, _, block, _ = own_hbm.shape
    def weight_loads(kind, to):
        loads = []
        for side, (source, parity) in enumerate(((own_hbm, core), (other_hbm, 1 - core))):
            for chip in range(chips):
                at = pl.ds(pl.multiple_of((2 * chip + parity) * block, block), block)
                loads.append(pltpu.make_async_copy(source.at[chip, kind], to.at[at], weight_sems.at[kind, side, chip]))
        return loads
    weights = [weight_loads(kind, to) for kind, to in enumerate((wo, wg, wu, wd))]
    for load in [loads[0]] + weights[0] + loads[1:] + weights[1] + weights[2] + weights[3]: load.start()
    gsum_ref[...] = jnp.zeros_like(gsum_ref)
    enter()
    for load in [loads[0]] + weights[0]: load.wait()
    def project(index, carry):
        k, flow = index // 2, index % 2
        at = pl.ds(pl.multiple_of(flow * half + k * big, big), big)
        part1[at, :] = dot(y[at, :], wo[...], ((1,), (1,))).astype(bfloat)
        @pl.when(one.near(flow) == 0)
        def _():
            one.reduce(flow, 2 * k)
            one.reduce(flow, 2 * k + 1)
        return carry
    lax.fori_loop(0, count, project, 0)
    for load in loads[1:] + weights[1] + weights[2] + weights[3]: load.wait()
    outs = ((n2s, n2_hbm), (ms, m_hbm), (das, da_hbm), (dbs, db_hbm), (pds, pd_hbm))
    def out_copy(i, flow, at):
        return pltpu.make_async_copy(outs[i][0].at[flow], outs[i][1].at[at], out_sems.at[i, flow])
    def dh_copy(flow, at):
        return pltpu.make_async_copy(dhs.at[flow], dh_hbm.at[at], out_sems.at[5, flow])
    def dy_copy(flow, at):
        return pltpu.make_async_copy(dys.at[flow], dy_hbm.at[at], out_sems.at[6, flow])

    def normed(at):
        mixed = x[at, :].astype(single) + land1[at, :].astype(single)
        rho = lax.rsqrt(jnp.mean(mixed * mixed, axis=-1, keepdims=True) + 1e-06)
        return rho, mixed * rho

    def inner(flow, k):
        at = pl.ds(pl.multiple_of(flow * half + k * big, big), big)
        @pl.when(k > 0)
        def _():
            for i in range(5): out_copy(i, flow, at).wait()
        rho, standard = normed(at)
        n2 = (standard * gain_ref[...]).astype(bfloat)
        n2s[flow] = n2
        a = dot(n2, wg[...], ((1,), (0,)))
        b = dot(n2, wu[...], ((1,), (0,)))
        dm = dot(g[at, :], wd[...], ((1,), (0,)))
        phi = 0.5 * (1.0 + lax.erf(a * math.sqrt(0.5)))
        gelu = a * phi
        slope = phi + a * jnp.exp(-0.5 * a * a) * (1.0 / math.sqrt(2.0 * math.pi))
        m = (gelu * b).astype(bfloat)
        da = (dm * b * slope).astype(bfloat)
        db = (dm * gelu).astype(bfloat)
        ms[flow] = m
        das[flow] = da
        dbs[flow] = db
        p3 = dot(da, wg[...], ((1,), (1,))) + dot(db, wu[...], ((1,), (1,)))
        part3[at, :] = p3.astype(bfloat)
        gsum_ref[...] += jnp.sum(p3 * standard, axis=0, keepdims=True)
        pds[flow] = dot(m, wd[...], ((1,), (1,))).astype(bfloat)
        for i in range(5): out_copy(i, flow, at).start()

    def last(flow, k):
        at = pl.ds(pl.multiple_of(flow * half + k * big, big), big)
        @pl.when(k > 0)
        def _():
            dh_copy(flow, at).wait()
            dy_copy(flow, at).wait()
        rho, standard = normed(at)
        scaled = land3[at, :].astype(single) * gain_ref[...]
        dh = g[at, :].astype(single) + rho * (
            scaled - standard * jnp.mean(scaled * standard, axis=-1, keepdims=True))
        low = dh.astype(bfloat)
        dhs[flow] = low
        dys[flow] = dot(low, wo[...], ((1,), (0,)))
        dh_copy(flow, at).start()
        dy_copy(flow, at).start()

    lag = 1
    slots = count + 4 * (n - 1) + lag + 1
    def slot(index, carry):
        s, flow = index // 2, index % 2
        near = one.near(flow)
        r = s - near
        @pl.when((near > 0) & (r >= 0) & (r < count))
        def _(): one.reduce(flow, r)
        arrival = 2 * (n - 1) - near
        k = s - arrival
        @pl.when((k >= 0) & (k < count))
        def _():
            one.cast(flow, k)
            @pl.when(k % 2 == 1)
            def _(): inner(flow, k // 2)
        near3 = n - 1 - near
        q = s - arrival - lag
        @pl.when((q >= 0) & (q < count) & (q % 2 == 1))
        def _():
            two.reduce(flow, q - 1)
            two.reduce(flow, q)
        e = s - (3 * (n - 1) - lag * 0) - (n - 1 - near3) - lag
        @pl.when((e >= 0) & (e < count) & (e % 2 == 1))
        def _():
            two.cast(flow, e - 1)
            two.cast(flow, e)
            last(flow, e // 2)
        return carry
    lax.fori_loop(0, 2 * slots, slot, 0)
    total_copy = pltpu.make_async_copy(land1, total_hbm, in_sems.at[0])
    total_copy.start()
    one.finish()
    two.finish()
    for flow in (0, 1):
        at = pl.ds(flow * half, big)
        for i in range(5): out_copy(i, flow, at).wait()
        dh_copy(flow, at).wait()
        dy_copy(flow, at).wait()
    total_copy.wait()

def middle(y, x, g, own, other, gain, cid, rows=64):
    full, width = x.shape
    hidden = y.shape[1]
    half = full // 2
    count = half // rows
    big = 2 * rows
    any_ = pl.BlockSpec(memory_space=pl.ANY)
    vm = pl.BlockSpec(memory_space=pltpu.VMEM)
    S = jax.ShapeDtypeStruct
    V = pltpu.VMEM
    wide, slim = (full, width), (full, hidden)
    return pl.pallas_call(
        functools.partial(middle_kernel, rows),
        out_shape=[S(wide, bfloat), S(wide, bfloat), S(slim, bfloat), S(slim, bfloat), S(slim, bfloat),
                   S(wide, bfloat), S(wide, bfloat), S(slim, single), S((1, width), single)],
        in_specs=[any_] * 5 + [vm],
        out_specs=[any_] * 8 + [vm],
        scratch_shapes=[V(slim, bfloat), V(wide, bfloat), V(wide, bfloat)] + [V((width, hidden), bfloat)] * 4
            + [V(wide, bfloat)] * 4
            + [V((2, big, width), bfloat), V((2, big, hidden), bfloat), V((2, big, hidden), bfloat),
               V((2, big, hidden), bfloat), V((2, big, width), bfloat), V((2, big, width), bfloat), V((2, big, hidden), single)]
            + [pltpu.SemaphoreType.DMA((3,)), pltpu.SemaphoreType.DMA((4, 2, own.shape[0])), pltpu.SemaphoreType.DMA((7, 2))]
            + [pltpu.SemaphoreType.DMA((2, count))] * 8,
        compiler_params=pltpu.CompilerParams(collective_id=cid, has_side_effects=True, vmem_limit_bytes=VMEM_ALL),
        cost_estimate=pl.CostEstimate(flops=260 * 10**9, bytes_accessed=60 * 10**6, transcendentals=0),
    )(y, x, g, own, other, gain)


def others():
    me = lax.axis_index("seq")
    core = me + 1 - 2 * (me % 2)
    x = 2 - 4 * ((me // 2) % 2)
    y = 4 - 8 * (me // 4)
    return core, (me + x, me + y, me + x + y)

def greet(devices):
    barrier = pltpu.get_barrier_semaphore()
    for device in devices:
        pl.semaphore_signal(barrier, inc=1, device_id={"seq": device}, device_id_type=MESH)
    pl.semaphore_wait(barrier, len(devices))

def scatter_kernel(shape, *refs):
    lefts = len(shape)
    matrices = [(g, i) for g, kinds in enumerate(shape) for i in range(kinds)]
    k = len(matrices)
    refs = list(refs)
    take = lambda count: [refs.pop(0) for _ in range(count)]
    left_hbm, right_hbm, outs = take(lefts), take(k), take(k)
    left, right = take(lefts), take(k)
    near_stage, near_land, far_stage, far_land = take(k), take(k), take(k), take(k)
    load_sem, near_send, near_recv, far_send, far_recv = refs
    loads = [pltpu.make_async_copy(a, b, load_sem.at[i])
             for i, (a, b) in enumerate(zip(left_hbm + right_hbm, left + right))]
    for load in loads: load.start()
    me = lax.axis_index("seq")
    core, chips = others()
    greet((core, *chips))
    rows = outs[0].shape[0]
    for load in loads: load.wait()

    def near_copy(i, r):
        return pltpu.make_async_remote_copy(
            src_ref=near_stage[i].at[r], dst_ref=near_land[i].at[r], send_sem=near_send.at[i, r],
            recv_sem=near_recv.at[i, r], device_id={"seq": core}, device_id_type=MESH)
    def far_copy(i, r, device):
        return pltpu.make_async_remote_copy(
            src_ref=far_stage[i].at[r - 1], dst_ref=far_land[i].at[r - 1], send_sem=far_send.at[i, r - 1],
            recv_sem=far_recv.at[i, r - 1], device_id={"seq": device}, device_id_type=MESH)
    def away(r):
        x = 2 - 4 * ((me // 2) % 2)
        y = 4 - 8 * (me // 4)
        return (r % 2) * x + (r // 2) * y
    def block(g, device):
        columns = pl.ds(pl.multiple_of(device * rows, rows), rows)
        return left[g][:, columns].T
    def tiles(device, use):
        index = 0
        for g, kinds in enumerate(shape):
            turned = block(g, device)
            for _ in range(kinds):
                use(index, dot(turned, right[index][...], ((1,), (0,))))
                index += 1
    def step(t, carry):
        @pl.when(t < 4)
        def _():
            r = 3 - t
            def use(i, tile):
                near_stage[i][r] = tile.astype(bfloat)
                near_copy(i, r).start()
            tiles(core + away(r), use)
        @pl.when(t > 0)
        def _():
            r = 4 - t
            def use(i, tile):
                near_copy(i, r).wait_recv()
                pair = tile + near_land[i][r].astype(single)
                @pl.when(r > 0)
                def _():
                    far_stage[i][r - 1] = pair.astype(bfloat)
                    far_copy(i, r, me + away(r)).start()
                @pl.when(r == 0)
                def _(): outs[i][...] = pair
            tiles(me + away(r), use)
        return carry
    lax.fori_loop(0, 5, step, 0)
    for i in range(k):
        for r in (1, 2, 3): far_copy(i, r, me + away(r)).wait_recv()
        outs[i][...] += (far_land[i][0].astype(single) + far_land[i][1].astype(single)) + far_land[i][2].astype(single)
    for i in range(k):
        for r in range(4): near_copy(i, r).wait_send()
        for r in (1, 2, 3): far_copy(i, r, me + away(r)).wait_send()

def grads_scattered(groups, cid):
    shape = tuple(len(rights) for _, rights in groups)
    lefts = [left for left, _ in groups]
    rights = [right for _, rights in groups for right in rights]
    rows = lefts[0].shape[1] // lax.axis_size("seq")
    V = pltpu.VMEM
    any_ = pl.BlockSpec(memory_space=pl.ANY)
    vm = pl.BlockSpec(memory_space=pltpu.VMEM)
    k = len(rights)
    tile = lambda count: [V((count, rows, right.shape[1]), bfloat) for right in rights]
    return pl.pallas_call(
        functools.partial(scatter_kernel, shape),
        out_shape=[jax.ShapeDtypeStruct((rows, right.shape[1]), single) for right in rights],
        in_specs=[any_] * (len(lefts) + k),
        out_specs=[vm] * k,
        scratch_shapes=[V(a.shape, bfloat) for a in lefts + rights] + tile(4) + tile(4) + tile(3) + tile(3)
            + [pltpu.SemaphoreType.DMA((len(lefts) + k,)), pltpu.SemaphoreType.DMA((k, 4)), pltpu.SemaphoreType.DMA((k, 4)),
               pltpu.SemaphoreType.DMA((k, 3)), pltpu.SemaphoreType.DMA((k, 3))],
        compiler_params=pltpu.CompilerParams(collective_id=cid, has_side_effects=True, vmem_limit_bytes=VMEM_ALL),
        cost_estimate=pl.CostEstimate(flops=80 * 10**9, bytes_accessed=30 * 10**6, transcendentals=0),
    )(*lefts, *rights)


def orthogonal_kernel(x_ref, out_ref, current):
    height = x_ref.shape[0]
    piece = 256
    def total(i, carry):
        value = x_ref[pl.ds(pl.multiple_of(i * piece, piece), piece), :].astype(single)
        return carry + jnp.sum(value * value, axis=0, keepdims=True)
    squares = lax.fori_loop(0, height // piece, total, jnp.zeros((1, x_ref.shape[1]), single))
    norm = jnp.sqrt(jnp.sum(squares, axis=1, keepdims=True)) + 1e-07
    def start(i, carry):
        at = pl.ds(pl.multiple_of(i * piece, piece), piece)
        value = x_ref[at, :].astype(single) / norm
        current[at, :] = value
        out_ref[at, :] = value.astype(bfloat)
        return carry
    lax.fori_loop(0, height // piece, start, 0)
    def newton(step, carry):
        def gram(i, q):
            rounded = out_ref[pl.ds(pl.multiple_of(i * 512, 512), 512), :]
            return q + dot(rounded, rounded, ((0,), (0,)))
        q = lax.fori_loop(0, height // 512, gram, jnp.zeros((x_ref.shape[1],) * 2, single))
        low = q.astype(bfloat)
        poly = (coef_second * q + coef_third * dot(low, low, ((1,), (0,)))).astype(bfloat)
        def apply(i, carry):
            at = pl.ds(pl.multiple_of(i * piece, piece), piece)
            value = coef_first * current[at, :] + dot(out_ref[at, :], poly, ((1,), (0,)))
            current[at, :] = value
            out_ref[at, :] = value.astype(bfloat)
            return carry
        return lax.fori_loop(0, height // piece, apply, carry)
    lax.fori_loop(0, 5, newton, 0)

def orthogonal(block):
    vm = pl.BlockSpec(memory_space=pltpu.VMEM)
    return pl.pallas_call(
        orthogonal_kernel, out_shape=jax.ShapeDtypeStruct(block.shape, bfloat), in_specs=[vm], out_specs=vm,
        scratch_shapes=[pltpu.VMEM(block.shape, single)],
        compiler_params=pltpu.CompilerParams(vmem_limit_bytes=48 << 20),
        cost_estimate=pl.CostEstimate(flops=17 * 10**9, bytes_accessed=4 * 10**6, transcendentals=0),
    )(block)


def rotated(values, cosine, sine):
    width = values.shape[1]
    even = lax.broadcasted_iota(jnp.int32, values.shape, 1) % 2 == 0
    swapped = jnp.where(even, -pltpu.roll(values, width - 1, 1), pltpu.roll(values, 1, 1))
    return values * cosine + swapped * sine

def front_kernel(x_hbm, gain_ref, cos_ref, sin_ref, q_hbm, k_hbm, v_hbm, s_hbm,
                 q_full, k_full, v_full, s_full, gains, n1, qh, kh, vh, sh,
                 x, rho, wq, wk, wv, ws, fq, fk, fv, fs, aq, ak, av, as_, load_sem, store_sem, send_sem, recv_sem):
    masters = (q_hbm, v_hbm, k_hbm, s_hbm)
    singles = (fq, fv, fk, fs)
    lands = (wq, wv, wk, ws, gains)
    fulls = (q_full, v_full, k_full, s_full)
    accs = (aq, av, ak, as_)
    loads = [pltpu.make_async_copy(a, b, load_sem.at[i]) for i, (a, b) in enumerate(zip(masters + (x_hbm,), singles + (x,)))]
    for load in loads: load.start()
    me = lax.axis_index("seq")
    core, (by_x, by_y, by_both) = others()
    step = {1: 1 - 2 * (me % 2), 2: 2 - 4 * ((me // 2) % 2), 4: 4 - 8 * (me // 4)}
    def place(rel):
        return me + sum(step[bit] for bit in (1, 2, 4) if rel & bit)
    greet((core, by_x, by_y))
    sent = []
    def send(rel, i, to):
        there = lands[i].at[place(rel)]
        copy = pltpu.make_async_remote_copy(
            src_ref=there, dst_ref=there, send_sem=send_sem.at[rel ^ to, i, to // 2], recv_sem=recv_sem.at[rel ^ to, i],
            device_id={"seq": place(to)}, device_id_type=MESH)
        copy.start()
        sent.append(copy)
    def arrive(rel, i):
        here = lands[i].at[place(rel)]
        pltpu.make_async_remote_copy(
            src_ref=here, dst_ref=here, send_sem=send_sem.at[rel, i, 0], recv_sem=recv_sem.at[rel, i],
            device_id={"seq": core}, device_id_type=MESH).wait_recv()
    gains[me] = gain_ref[...].astype(bfloat).astype(single)
    for to in (2, 4, 1): send(0, 4, to)
    for i in range(4):
        loads[i].wait()
        lands[i][me] = singles[i][...].astype(bfloat)
        for to in (2, 4, 1): send(0, i, to)
    loads[4].wait()
    tokens = x.shape[0]
    piece = 256
    def scale(t, carry):
        at = pl.ds(pl.multiple_of(t * piece, piece), piece)
        value = x[at, :].astype(single)
        rho[at, :] = lax.rsqrt(jnp.mean(value * value, axis=-1, keepdims=True) + 1e-06)
        return carry
    lax.fori_loop(0, tokens // piece, scale, 0)
    rows = gain_ref.shape[1]
    def product(rel, first):
        low = place(rel) - me % 2
        columns = pl.ds(pl.multiple_of(low * rows, 2 * rows), 2 * rows)
        scales = jnp.concatenate([gains[low][0:1, :], gains[low + 1][0:1, :]], axis=1)
        weights = [lands[i][pl.ds(low, 2)].reshape(2 * rows, lands[i].shape[2]) for i in range(4)]
        def part(t, carry):
            at = pl.ds(pl.multiple_of(t * piece, piece), piece)
            normed = (x[at, columns].astype(single) * rho[at, :] * scales).astype(bfloat)
            n1[at, columns] = normed
            for i in range(4):
                value = dot(normed, lands[i][pl.ds(low, 2)].reshape(2 * rows, lands[i].shape[2]), ((1,), (0,)))
                if first: accs[i][at, :] = value
                else: accs[i][at, :] += value
            return carry
        lax.fori_loop(0, tokens // piece, part, 0)
    for i in (4, 0, 1, 2, 3): arrive(1, i)
    product(0, True)
    def relay(rel, i):
        arrive(rel, i)
        send(rel, i, 1)
        if rel == 2 and i in (0, 1, 4): send(rel, i, 4)
        if rel == 4 and i in (2, 3): send(rel, i, 2)
    for i in (4, 0, 1, 2, 3):
        relay(2, i)
        relay(4, i)
    for i in (4, 0, 1, 2, 3): arrive(3, i)
    product(2, False)
    for i in (4, 0, 1, 2, 3): arrive(5, i)
    product(4, False)
    for i in (4, 0, 2, 1, 3):
        arrive(6, i)
        send(6, i, 1)
    for i in (4, 0, 2, 1, 3): arrive(7, i)
    stores = [pltpu.make_async_copy(a, b, store_sem.at[i]) for i, (a, b) in enumerate(zip(lands[:4], fulls))]
    for store in stores: store.start()
    product(6, False)
    heads = qh.shape[0] // 2
    block = tokens // 2
    def finish(s, carry):
        at = pl.ds(pl.multiple_of(s * block, block), block)
        for h in range(heads):
            keys = slice(h * KEY, (h + 1) * KEY)
            qh[s * heads + h] = rotated(aq[at, keys], cos_ref[...], sin_ref[...]).astype(bfloat)
            kh[s * heads + h] = (rotated(ak[at, keys], cos_ref[...], sin_ref[...]) * KEY ** -0.5).astype(bfloat)
            vh[s * heads + h] = av[at, :][:, h * VAL : (h + 1) * VAL].astype(bfloat)
            sh[s * heads + h] = as_[at, :][:, h * VAL : (h + 1) * VAL]
        return carry
    lax.fori_loop(0, 2, finish, 0)
    for copy in sent: copy.wait_send()
    for store in stores: store.wait()

def front(x, gains, cosine, sine, wq, wk, wv, ws, cid):
    tokens, width = x.shape
    count = lax.axis_size("seq")
    rows = width // count
    block = tokens // 2
    heads = wq.shape[1] // KEY
    any_ = pl.BlockSpec(memory_space=pl.ANY)
    vm = pl.BlockSpec(memory_space=pltpu.VMEM)
    S, V = jax.ShapeDtypeStruct, pltpu.VMEM
    gathered = [(count, rows, w.shape[1]) for w in (wq, wk, wv, ws)]
    return pl.pallas_call(
        front_kernel,
        out_shape=[S(g, bfloat) for g in gathered] + [S((count, 8, rows), single), S(x.shape, bfloat),
            S((2 * heads, block, KEY), bfloat), S((2 * heads, block, KEY), bfloat), S((2 * heads, block, VAL), bfloat), S((2 * heads, block, VAL), single)],
        in_specs=[any_, vm, vm, vm] + [any_] * 4,
        out_specs=[any_] * 4 + [vm] * 6,
        scratch_shapes=[V(x.shape, bfloat), V((tokens, 1), single)] + [V(g, bfloat) for g in gathered]
            + [V(w.shape, single) for w in (wq, wk, wv, ws)] + [V((tokens, w.shape[1]), single) for w in (wq, wk, wv, ws)]
            + [pltpu.SemaphoreType.DMA((5,)), pltpu.SemaphoreType.DMA((4,)), pltpu.SemaphoreType.DMA((8, 5, 3)), pltpu.SemaphoreType.DMA((8, 5))],
        compiler_params=pltpu.CompilerParams(collective_id=cid, has_side_effects=True, vmem_limit_bytes=VMEM_ALL),
        cost_estimate=pl.CostEstimate(flops=70 * 10**9, bytes_accessed=40 * 10**6, transcendentals=0),
    )(x, gains, cosine, sine, wq, wk, wv, ws)


def peers():
    me = lax.axis_index("seq")
    core, (by_x, by_y, by_both) = others()
    turn = core - me
    return core, by_x, by_y, by_x + turn, by_y + turn, by_both, by_both + turn

def decays(rate, length):
    t = lax.broadcasted_iota(jnp.int32, (length, 1), 0).astype(single)
    u = lax.broadcasted_iota(jnp.int32, (1, length), 1).astype(single)
    offsets = t - u
    mask = jnp.where(offsets >= 0, jnp.exp(-rate * jnp.maximum(offsets, 0.0)), 0.0)
    return mask, jnp.exp(-rate * (t + 1.0)), jnp.exp(-rate * (length - 1.0 - t)), jnp.exp(-rate * length)

class Exchange:
    def __init__(self, stage, land, stage_two, land_two, sems):
        self.stage, self.land, self.stage_two, self.land_two = stage, land, stage_two, land_two
        self.sends, self.recvs, self.sends_two, self.recvs_two = sems
        self.me = lax.axis_index("seq")
        self.peers = peers()
    def copy(self, two, i):
        stage, land = (self.stage_two, self.land_two) if two else (self.stage, self.land)
        sends, recvs = (self.sends_two, self.recvs_two) if two else (self.sends, self.recvs)
        return pltpu.make_async_remote_copy(
            src_ref=stage.at[self.peers[i]], dst_ref=land.at[self.me], send_sem=sends.at[i],
            recv_sem=recvs.at[i], device_id={"seq": self.peers[i]}, device_id_type=MESH)
    def arrived(self, two, i):
        land = self.land_two if two else self.land
        recvs = self.recvs_two if two else self.recvs
        sends = self.sends_two if two else self.sends
        here = land.at[self.peers[i]]
        pltpu.make_async_remote_copy(
            src_ref=here, dst_ref=here, send_sem=sends.at[i], recv_sem=recvs.at[i],
            device_id={"seq": self.peers[i]}, device_id_type=MESH).wait_recv()
    def start(self):
        for i in reversed(range(7)): self.copy(False, i).start()
        self.land[self.me] = self.stage[self.me]
    def turn(self, decay, reverse):
        for i in range(7): self.arrived(False, i)
        count = self.stage.shape[0]
        def step(index, running):
            position = count - 1 - index if reverse else index
            self.stage_two[position] = running.astype(bfloat)
            return decay * running + self.land[position].astype(single)
        lax.fori_loop(0, count, step, jnp.zeros(self.stage.shape[1:], single))
        for i in reversed(range(7)): self.copy(True, i).start()
        self.land_two[self.me] = self.stage_two[self.me]
    def end(self):
        for i in range(7): self.arrived(True, i)
    def state(self, b):
        count, _, part, width = self.land_two.shape
        return self.land_two[:, b].reshape(count * part, width)
    def finish(self):
        for i in range(7):
            self.copy(False, i).wait_send()
            self.copy(True, i).wait_send()

def retain_kernel(heads, q, k, v, s, rates, y, o, weights, state, stage, land, stage_two, land_two, *sems):
    blocks, length = q.shape[0], q.shape[1]
    count = stage.shape[0]
    exchange = Exchange(stage, land, stage_two, land_two, sems)
    greet(exchange.peers)
    rate = lambda h: rates[pl.ds(h, 1), 0:1]
    def local(b, carry):
        _, _, kd, _ = decays(rate(b % heads), length)
        low = (k[b].astype(single) * kd).astype(bfloat)
        piece = dot(low, v[b], ((0,), (0,))).astype(bfloat)
        stage[:, pl.ds(b, 1)] = piece.reshape(count, 1, piece.shape[0] // count, piece.shape[1])
        return carry
    lax.fori_loop(0, blocks, local, 0)
    exchange.start()
    def inside(b, carry):
        mask, _, _, _ = decays(rate(b % heads), length)
        low = (dot(q[b], k[b], ((1,), (1,))) * mask).astype(bfloat)
        weights[b] = low
        o[b] = dot(low, v[b], ((1,), (0,)))
        return carry
    lax.fori_loop(0, blocks, inside, 0)
    head = lax.broadcasted_iota(jnp.int32, (blocks, 1, 1), 0) % heads
    whole = jnp.zeros((blocks, 1, 1), single)
    for h in range(heads):
        whole = jnp.where(head == h, jnp.exp(-rate(h) * length).reshape(1, 1, 1), whole)
    exchange.turn(whole, False)
    exchange.end()
    def outer(sequence, carry):
        parts = []
        for h in range(heads):
            b = sequence * heads + h
            _, qd, _, _ = decays(rate(h), length)
            incoming = exchange.state(b)
            state[b] = incoming
            total = o[b] + dot((q[b].astype(single) * qd).astype(bfloat), incoming, ((1,), (0,)))
            o[b] = total
            rho = lax.rsqrt(jnp.mean(total * total, axis=-1, keepdims=True) + 1e-05)
            gate = s[b]
            parts.append((gate * jax.nn.sigmoid(gate) * total * rho).astype(bfloat))
        at = pl.ds(pl.multiple_of(sequence * length, length), length)
        y[at, :] = jnp.concatenate(parts, axis=1)
        return carry
    lax.fori_loop(0, blocks // heads, outer, 0)
    exchange.finish()

def exchange_scratch(count, blocks, keys, vals):
    return [pltpu.VMEM((count, blocks, keys // count, vals), bfloat)] * 4 + [pltpu.SemaphoreType.DMA((7,))] * 4

def retain(q, k, v, s, rates, cid):
    blocks, length, keys = q.shape
    vals = v.shape[2]
    heads = rates.shape[0]
    count = lax.axis_size("seq")
    vm = pl.BlockSpec(memory_space=pltpu.VMEM)
    S = jax.ShapeDtypeStruct
    return pl.pallas_call(
        functools.partial(retain_kernel, heads),
        out_shape=[S((blocks // heads * length, heads * vals), bfloat), S((blocks, length, vals), single),
                   S((blocks, length, length), bfloat), S((blocks, keys, vals), bfloat)],
        in_specs=[vm] * 5, out_specs=[vm] * 4,
        scratch_shapes=exchange_scratch(count, blocks, keys, vals),
        compiler_params=pltpu.CompilerParams(collective_id=cid, has_side_effects=True, vmem_limit_bytes=48 << 20),
        cost_estimate=pl.CostEstimate(flops=40 * 10**9, bytes_accessed=20 * 10**6, transcendentals=0),
    )(q, k, v, s, jnp.broadcast_to(rates[:, None], (heads, 128)))

def scattered_products(groups, cid):
    if lax.axis_size("seq") == 8:
        return grads_scattered(groups, cid)
    sums = []
    for left, rights in groups:
        for right in rights:
            sums.append(scattered([tn(left, right)])[0])
    return sums


def by_block(array, heads):
    rows, columns = array.shape
    parts = array.reshape(SEQS, rows // SEQS, heads, columns // heads).transpose(0, 2, 1, 3)
    return parts.reshape(SEQS * heads, rows // SEQS, columns // heads)


def by_row(array):
    blocks, length, columns = array.shape
    heads = blocks // SEQS
    parts = array.reshape(SEQS, heads, length, columns).transpose(0, 2, 1, 3)
    return parts.reshape(SEQS * length, heads * columns)


def rotate(values, cosine, sine):
    column = lax.broadcasted_iota(jnp.int32, values.shape, values.ndim - 1)
    swapped = jnp.where(
        column % 2 == 0, -jnp.roll(values, -1, axis=-1), jnp.roll(values, 1, axis=-1)
    )
    return values * cosine + swapped * sine


def projected(x, retention_gain, channel_gain, cosine, sine, weights):
    width = x.shape[1]
    heads = HEADS // lax.axis_size("head")
    gains = jnp.stack([retention_gain, channel_gain])
    if lax.axis_size("seq") == 8:
        gains = jnp.pad(gains, ((0, 6), (0, 0)))
        *fulls, gains, normed, q, k, v, s = front(x, gains, cosine, sine, *weights, 3)
        fulls = [full.reshape(width, full.shape[2]) for full in fulls]
        return fulls, (gains[:, 0].reshape(-1), gains[:, 1].reshape(-1)), normed, (q, k, v, s)
    gains = lax.all_gather(gains.astype(bfloat), "seq", axis=1, tiled=True).astype(single)
    fulls = gathered(jnp.stack([weights[0].astype(bfloat), weights[1].astype(bfloat)]))
    fulls += gathered(jnp.stack([weights[2].astype(bfloat), weights[3].astype(bfloat)]))
    stream = x.astype(single)
    rho = lax.rsqrt(jnp.mean(stream * stream, axis=-1, keepdims=True) + 1e-06)
    normed = (stream * rho * gains[0]).astype(bfloat)
    q, k, v, s = [by_block(nn(normed, full), heads) for full in fulls]
    q = rotate(q, cosine, sine).astype(bfloat)
    k = (rotate(k, cosine, sine) * KEY ** (-0.5)).astype(bfloat)
    return fulls, (gains[0], gains[1]), normed, (q, k, v.astype(bfloat), s)


def factors(rates, length):
    steps = jnp.arange(length, dtype=single)
    offsets = steps[:, None] - steps[None, :]
    every = jnp.tile(rates, SEQS)[:, None, None]
    mask = jnp.where(offsets >= 0, jnp.exp(-every * jnp.maximum(offsets, 0.0)), 0.0)
    steps = steps[None, :, None]
    return mask, jnp.exp(-every * (steps + 1.0)), jnp.exp(-every * (length - 1.0 - steps)), jnp.exp(-every * length)


def batched(spec, left, right):
    return jnp.einsum(spec, left, right, preferred_element_type=single)


def retained(q, k, v, s, rates):
    if lax.axis_size("seq") == 8:
        return retain(q, k, v, s, rates, 4)
    mask, qd, kd, whole = factors(rates, q.shape[1])
    local = batched("buk,buv->bkv", (k.astype(single) * kd).astype(bfloat), v)
    incoming = state_exchange(local, whole, False)
    weights = (batched("btk,buk->btu", q, k) * mask).astype(bfloat)
    o = batched("btu,buv->btv", weights, v)
    o = o + batched("btk,bkv->btv", (q.astype(single) * qd).astype(bfloat), incoming)
    rho = lax.rsqrt(jnp.mean(o * o, axis=-1, keepdims=True) + 1e-05)
    gated = (s * jax.nn.sigmoid(s) * o * rho).astype(bfloat)
    return by_row(gated), o, weights, incoming


def unretained(gated_grad, q, k, v, s, o, weights, incoming, rates, cosine, sine):
    heads = rates.shape[0]
    mask, qd, kd, whole = factors(rates, q.shape[1])
    grad = by_block(gated_grad, heads)
    rho = lax.rsqrt(jnp.mean(o * o, axis=-1, keepdims=True) + 1e-05)
    sigmoid = jax.nn.sigmoid(s)
    ds = (grad * (o * rho) * (sigmoid * (1.0 + s * (1.0 - sigmoid)))).astype(bfloat)
    inner = grad * (s * sigmoid)
    do = (
        rho * (inner - o * (rho * rho * jnp.mean(inner * o, axis=-1, keepdims=True)))
    ).astype(bfloat)
    local = batched("btk,btv->bkv", (q.astype(single) * qd).astype(bfloat), do)
    outgoing = state_exchange(local, whole, True)
    score = (batched("btv,buv->btu", do, v) * mask).astype(bfloat)
    dv = batched("btu,btv->buv", weights, do)
    dv = dv + batched("buk,bkv->buv", (k.astype(single) * kd).astype(bfloat), outgoing)
    dq = batched("btu,buk->btk", score, k) + batched("btv,bkv->btk", do, incoming) * qd
    dk = batched("btu,btk->buk", score, q) + batched("buv,bkv->buk", v, outgoing) * kd
    dq = rotate(dq, cosine, -sine).astype(bfloat)
    dk = (rotate(dk, cosine, -sine) * KEY ** (-0.5)).astype(bfloat)
    return by_row(dq), by_row(dk), by_row(dv.astype(bfloat)), by_row(ds)


def shards(
    tokens,
    cotangent,
    decay_rates,
    retention_gain,
    channel_gain,
    query_weight,
    key_weight,
    value_weight,
    swish_weight,
    output_weight,
    gate_weight,
    up_weight,
    down_weight,
    query_moment,
    key_moment,
    value_moment,
    swish_moment,
    output_moment,
    gate_moment,
    up_moment,
    down_moment,
    retention_first,
    retention_second,
    channel_first,
    channel_second,
):
    heads_here = HEADS // lax.axis_size("head")
    seq_count, block_length, width = tokens.shape
    rows = seq_count * block_length
    own_four = chips_gathered(
        jnp.stack(
            [
                output_weight.astype(bfloat).T,
                gate_weight.astype(bfloat),
                up_weight.astype(bfloat),
                down_weight.astype(bfloat).T,
            ]
        )
    )
    upstream_low = cotangent.reshape(rows, width)
    positions = (lax.axis_index("seq") * block_length + jnp.arange(block_length)).astype(single)
    pair_index = (jnp.arange(KEY) // 2).astype(single)
    frequency = jnp.exp(-log_base * pair_index / (KEY // 2 - 1))
    angles = positions[:, None] * frequency[None, :]
    cosine, sine = jnp.cos(angles), jnp.sin(angles)
    rates = lax.dynamic_slice(decay_rates, (lax.axis_index("head") * heads_here,), (heads_here,))
    (
        (query_full, key_full, value_full, swish_full),
        (retention_scale, channel_scale),
        normed_low,
        (query_blocks, key_blocks, value_blocks, swish_blocks),
    ) = projected(
        tokens.reshape(rows, width),
        retention_gain,
        channel_gain,
        cosine,
        sine,
        [query_weight, key_weight, value_weight, swish_weight],
    )
    own_four, query_blocks = lax.optimization_barrier((own_four, query_blocks))
    other_four = sibling(own_four)
    gated_low, retained_blocks, weights_low, incoming_low = retained(
        query_blocks, key_blocks, value_blocks, swish_blocks, rates
    )
    stream = tokens.reshape(rows, width).astype(single)
    rho_one = lax.rsqrt(jnp.mean(stream * stream, axis=-1, keepdims=True) + 1e-06)
    (
        mixed_total,
        normed_two_low,
        activated_low,
        gate_low_grad,
        up_low_grad,
        down_partial,
        mixed_low,
        gated_grad,
        channel_local,
    ) = middle(
        gated_low,
        tokens.reshape(rows, width),
        upstream_low,
        own_four,
        other_four,
        channel_scale[None, :],
        1,
    )
    channel_sum = gain_total(channel_local[0])
    down_total = heads_total(down_partial)
    block_out = (stream + mixed_total.astype(single) + down_total).astype(bfloat)
    down_local = tn(upstream_low, activated_low)
    gate_local = tn(normed_two_low, gate_low_grad)
    up_local = tn(normed_two_low, up_low_grad)
    output_local = tn(mixed_low, gated_low)
    early = scattered([output_local, gate_local, up_local, down_local])
    query_low_grad, key_low_grad, value_low_grad, swish_low_grad = unretained(
        gated_grad,
        query_blocks,
        key_blocks,
        value_blocks,
        swish_blocks,
        retained_blocks,
        weights_low,
        incoming_low,
        rates,
        cosine,
        sine,
    )
    normed_one_partial = (
        nt(query_low_grad, query_full)
        + nt(key_low_grad, key_full)
        + nt(value_low_grad, value_full)
        + nt(swish_low_grad, swish_full)
    )
    late = scattered_products(
        [(normed_low, [query_low_grad, key_low_grad, value_low_grad, swish_low_grad])], 2
    )
    standard_one = stream * rho_one
    retention_sum = gain_total(jnp.sum(normed_one_partial * standard_one, axis=0))
    normed_one_partial, down_total = lax.optimization_barrier((normed_one_partial, down_total))
    block_out = (stream + mixed_total.astype(single) + down_total).astype(bfloat)
    normed_one_grad = heads_total(normed_one_partial)
    scaled_one = normed_one_grad * retention_scale
    input_gradient = (
        mixed_low.astype(single)
        + rho_one
        * (scaled_one - standard_one * jnp.mean(scaled_one * standard_one, axis=-1, keepdims=True))
    ).astype(bfloat)

    retention_gain_updated, retention_first_updated, retention_second_updated = adam_gain(
        retention_gain, retention_sum, retention_first, retention_second
    )
    channel_gain_updated, channel_first_updated, channel_second_updated = adam_gain(
        channel_gain, channel_sum, channel_first, channel_second
    )
    early_grads, early_moments, early_updated = muon_group(
        [early[0], early[1], early[2], early[3]],
        [output_moment, gate_moment, up_moment, down_moment],
        [output_weight, gate_weight, up_weight, down_weight],
        [VAL, FBLK, FBLK, FBLK],
        [True, False, False, True],
        0,
    )
    late_grads, late_moments, late_updated = muon_group(
        late,
        [query_moment, key_moment, value_moment, swish_moment],
        [query_weight, key_weight, value_weight, swish_weight],
        [KEY, KEY, VAL, VAL],
        [False, False, False, False],
        1,
    )
    whole = (seq_count, block_length, width)
    return (
        block_out.reshape(whole),
        input_gradient.reshape(whole),
        retention_sum,
        channel_sum,
        *late_grads,
        *early_grads,
        retention_gain_updated,
        channel_gain_updated,
        *late_updated,
        *early_updated,
        *late_moments,
        *early_moments,
        retention_first_updated,
        retention_second_updated,
        channel_first_updated,
        channel_second_updated,
    )


def solution(mesh):
    placed = (
        P(None, "seq", None),
        P(None, "seq", None),
        P(),
        P("seq"),
        P("seq"),
        P("seq", "head"),
        P("seq", "head"),
        P("seq", "head"),
        P("seq", "head"),
        P("head", "seq"),
        P("seq", "head"),
        P("seq", "head"),
        P("head", "seq"),
        P("seq", "head"),
        P("seq", "head"),
        P("seq", "head"),
        P("seq", "head"),
        P("head", "seq"),
        P("seq", "head"),
        P("seq", "head"),
        P("head", "seq"),
        P("seq"),
        P("seq"),
        P("seq"),
        P("seq"),
    )
    return jax.shard_map(
        shards,
        mesh=mesh,
        in_specs=placed,
        out_specs=(
            P(None, "seq", None),
            P(None, "seq", None),
            P("seq"),
            P("seq"),
            P("seq", "head"),
            P("seq", "head"),
            P("seq", "head"),
            P("seq", "head"),
            P("head", "seq"),
            P("seq", "head"),
            P("seq", "head"),
            P("head", "seq"),
            P("seq"),
            P("seq"),
            P("seq", "head"),
            P("seq", "head"),
            P("seq", "head"),
            P("seq", "head"),
            P("head", "seq"),
            P("seq", "head"),
            P("seq", "head"),
            P("head", "seq"),
            P("seq", "head"),
            P("seq", "head"),
            P("seq", "head"),
            P("seq", "head"),
            P("head", "seq"),
            P("seq", "head"),
            P("seq", "head"),
            P("head", "seq"),
            P("seq"),
            P("seq"),
            P("seq"),
            P("seq"),
        ),
        check_vma=False,
    )
```

time: 2330 us -> 1160 us (0.50)
  waiting for transfers between devices: 1560 us -> 74 us
  Pallas kernels: 0 us -> 535 us
  matrix products: 308 us -> 81.1 us
  local copies, waits for them, and re-layouts: 52.6 us -> 259 us
  starting transfers between devices: 166 us -> 33.2 us
  blocking collectives: 76.7 us -> 9.63 us
    psum x3 -> x2, waiting for transfers between devices: 949 us -> 61.7 us  [heads_total(): return lax.psum(partial_sum.astype(bfloat), 'head').astype(single)]
    pallas_call x0 -> x6, Pallas kernels: none -> 535 us  [the longest x1 244 us: middle(): pl.pallas_call(functools.partial(middle_kernel, rows), out_shape=[S(wide,...]
    reduce_scatter x8 -> x0, waiting for transfers between devices: 235 us -> none  [the longest x1 66.8 us: shards(): lax.psum_scatter(swish_local, 'seq', scatter_dimension=0, tiled=True)]
    dot_general x46 -> x16, matrix products: 308 us -> 81.1 us  [the longest x8 62.2 us: mm(): lax.dot_general(left, right, (contract, ((), ())), preferred_element_type...]
    ppermute x14 -> x2, waiting for transfers between devices: 218 us -> 0.01 us  [sibling(): return lax.ppermute(array, 'seq', [(i, i ^ 1) for i in range(count)])]
    ppermute x14 -> x2, starting transfers between devices: 156 us -> 0.27 us  [sibling(): return lax.ppermute(array, 'seq', [(i, i ^ 1) for i in range(count)])]
    all_gather x8 -> x1, waiting for transfers between devices: 118 us -> 5.13 us  [chips_gathered(): lax.all_gather(stacked, 'seq', axis=0, axis_index_groups=core_groups())]
    reshape x5 -> x15, local copies, waits for them, and re-layouts: 4.12 us -> 69.2 us  [the longest x4 41.8 us: scattered(): array.reshape(count // 2, 2, array.shape[0] // count, array.shape[1])]
  transfers between devices with their start and end apart: 35 -> 14, of which waited for: 28 -> 4; matrix products, arithmetic and copies ran while one was open for 18% -> 34% of each run, Pallas kernels for 0% -> 25%
where the time goes in v1:
time: 1160 us; the launch traced here: 1140 us
  Pallas kernels  535 us (46%)
  local copies, waits for them, and re-layouts  259 us (22%)
  other arithmetic  134 us (12%)
  matrix products  81.1 us (7%)
  waiting for transfers between devices  74 us (6%)
  starting transfers between devices  33.2 us (3%)
  between operations  15.1 us (1%)
    pallas_call x1, Pallas kernels, middle(): pl.pallas_call(functools.partial(middle_kernel, rows), out_shape=[S(wide,...  244 us
    pallas_call x1, Pallas kernels, front(): pl.pallas_call(front_kernel, out_shape=[S(g, bfloat) for g in gathered] +...  105 us
    pallas_call x1, Pallas kernels, grads_scattered(): pl.pallas_call(functools.partial(scatter_kernel, shape), out_shape=[jax.S...  96.5 us
    unnamed x197, local copies, waits for them, and re-layouts  69 us
    dot_general x8, matrix products, mm(): lax.dot_general(left, right, (contract, ((), ())), preferred_element_type...  62.2 us
    psum x2, waiting for transfers between devices, heads_total(): return lax.psum(partial_sum.astype(bfloat), 'head').astype(single)  61.7 us
    pallas_call x2, Pallas kernels, orthogonal(): pl.pallas_call(orthogonal_kernel, out_shape=jax.ShapeDtypeStruct(block.sh...  51.4 us
    slice x4, local copies, waits for them, and re-layouts, scattered(): own.append(jnp.where(second, parts[:, 1], parts[:, 0]))  42.5 us
  transfers between devices with their start and end apart: 14, of which 4 were waited for; matrix products, arithmetic and copies ran while one was open for 34% of the time, Pallas kernels for 25%

profile of v1, /device:TPU:0, one launch (start us, length us, event | category | flops | bytes accessed | tf_op | source)
XLA Modules:
  0.0 1140.8 jit_solution(8263174534731405187)
XLA Ops:
  15.0 3.1 fusion.39
  18.1 104.8 %shard_map.504 = (bf16[8,256,512]{2,1,0:T(8,128)(2,1)}, bf16[8,256,512]{2,1,0:T(8,128)(2,1)}, bf16[8,256,864]{2,1,0:T(8,128)(2,1)}, bf16[8,256,864]{2,1,0:T(8,12...) custom-call(bf16[1024,2048]{1,0:T(8,128)(2,1)} %bitcast.233, ...), custom_call_target="tpu_custom_call" | custom-call | flops 70000001024 | bytes 40000000 | tf_op jit(solution)/shard_map/pallas_call | solution.py:673
  122.9 5.1 all-gather.3.cloned.1.call-done
  128.1 11.1 copy.335
  139.2 10.8 copy.338
  159.9 38.0 %shard_map.505 = (bf16[1024,864]{1,0:T(8,128)(2,1)S(1)}, f32[4,512,432]{2,1,0:T(8,128)}, bf16[4,512,512]{2,1,0:T(8,128)(2,1)}, bf16[4,256,432]{2,1,0:T(8,128)(2,1)S(1)}) custom-call(bf16[4,512,256]{2,1,0:T(8,128)(2,1)S(1)} %copy-done.2, bf16[4,512,256]{2,1,0:T(8,128)(2,1)S(1)} %copy-done, bf16[4,512,432]{2,1,0:T(8,128)(2,1)} %get-tuple-element.68.v, ...), custom_call_target="tpu_custom_call" | custom-call | flops 40000000000 | bytes 20000000 | tf_op jit(solution)/shard_map/pallas_call | solution.py:798
  200.2 10.8 copy.339.other_hbm
  211.0 244.2 %shard_map.506 = (bf16[1024,2048]{1,0:T(8,128)(2,1)}, bf16[1024,2048]{1,0:T(8,128)(2,1)}, bf16[1024,864]{1,0:T(8,128)(2,1)}, bf16[1024,864]{1,0:T(8,128)(2,1)}, ...) custom-call(bf16[1024,864]{1,0:T(8,128)(2,1)} %copy-done.8, ...), custom_call_target="tpu_custom_call" | custom-call | flops 260000006144 | bytes 60000000 | tf_op jit(solution)/shard_map/pallas_call | solution.py:396
  455.2 7.5 reshape.480
  462.7 3.1 copy.341
  469.6 3.9 multiply_convert_fusion.1
  480.0 4.2 all-to-all-start
  485.0 9.6 convolution_bitcast_fusion
  494.5 10.7 reshape.462
  505.2 11.1 fusion.55
  516.3 5.9 fusion.72
  522.2 10.4 reshape.461
  532.5 11.1 fusion.54
  543.7 5.9 fusion.71
  549.5 10.4 reshape.460
  560.0 11.3 fusion.53
  571.3 5.9 fusion.70
  577.2 10.3 reshape.459
  587.5 9.0 fusion.52
  608.0 6.4 pad_maximum_fusion
  614.7 4.8 multiply_convert_fusion
  619.5 4.0 fusion.66
  626.9 2.9 fusion.67
  629.9 2.9 copy_select_fusion
  632.8 2.9 copy_select_fusion.1
  635.7 2.9 copy_select_fusion.2
  638.7 2.9 copy_select_fusion.3
  644.2 6.1 copy.363
  650.4 3.2 copy.442
  653.6 3.9 copy.367.refs_4_
  657.5 10.4 fusion.69
  675.3 4.2 all-to-all-start.1
  679.6 10.2 fusion
  691.6 3.4 all-to-all-done.1
  696.3 3.0 add_convert_fusion
  716.6 96.5 %shard_map.507 = (f32[256,512]{1,0:T(8,128)}, f32[256,512]{1,0:T(8,128)}, f32[256,864]{1,0:T(8,128)}, f32[256,864]{1,0:T(8,128)}) custom-call(bf16[1024,2048]{1,0:T(8,128)(2,1)} %get-tuple-element.87.refs_0_, bf16[1024,512]{1,0:T(8,128)(2,1)} %bitcast.268, bf16[1024,512]{1,0:T(8,128)(2,1)} %bitcast.248, bf16[1024,864]{1,0:T(8,128)(2,1)} %copy.366.refs_3_, ...), custom_call_target="tpu_custom_call" | custom-call | flops 80000000000 | bytes 30000000 | tf_op jit(solution)/shard_map/pallas_call | solution.py:507
  824.9 4.0 all-to-all-start.4
  828.9 6.8 fusion.68
  835.7 5.6 fusion.65
  841.3 12.3 %add_add_fusion = f32[1024,2048]{1,0:T(8,128)} fusion(f32[1024,2048]{1,0:T(8,128)} %fusion.69, f32[1024,2048]{1,0:T(8,128)S(1)} %fusion.68, f32[1024,2048]{1,0:T(8,128)} %fusion.65, bf16[1024,512]{1,0:T(8,128)(2,1)S(1)} %bitcast.249, bf16[2048,512]{1,0:T(8,128)(2,1)S(1)} %bitcast.257), kind=kOutput, calls=%fused_computation.17 | convolution fusion | flops 2153775104 | bytes 36700160 | tf_op jit(solution)/shard_map/dot_general | solution.py:33
  853.6 4.2 all-to-all-start.3
  860.6 6.6 convert_element_type.213
  867.2 6.0 convert_element_type.217
  873.3 25.7 %shard_map.508 = bf16[2048,432]{1,0:T(8,128)(2,1)S(1)} custom-call(bf16[2048,432]{1,0:T(8,128)(2,1)S(1)} %bitcast.229), custom_call_target="tpu_custom_call" | custom-call | flops 16999999488 | bytes 4000000 | tf_op jit(solution)/shard_map/pallas_call | solution.py:553
  900.3 4.0 copy.385
  904.3 4.5 all-to-all-start.5
  908.8 3.2 multiply_reduce_fusion
  928.9 2.9 all-to-all-done.5
  945.3 3.1 multiply_add_fusion.3
  953.5 3.6 all-to-all-start.6
  968.3 61.7 %all-reduce.10.cloned.1.call-done = bf16[1024,2048]{1,0:T(8,128)(2,1)} async-done(((bf16[1024,2048]{1,0:T(8,128)(2,1)}), bf16[1024,2048]{1,0:T(8,128)(2,1)}) %all-reduce.10.cloned.1.call-update) | async-done | bytes 4194320 | tf_op jit(solution)/shard_map/psum | solution.py:95
  1030.0 7.7 fusion.9
  1039.0 3.7 all-to-all-start.2
  1045.4 25.7 %shard_map.509 = bf16[2048,432]{1,0:T(8,128)(2,1)S(1)} custom-call(bf16[2048,432]{1,0:T(8,128)(2,1)S(1)} %bitcast.231), custom_call_target="tpu_custom_call" | custom-call | flops 16999999488 | bytes 4000000 | tf_op jit(solution)/shard_map/pallas_call | solution.py:553
  1072.4 3.9 copy.398
  1076.3 4.4 all-to-all-start.7
  1080.9 13.2 %fusion.8 = (bf16[1024,2048]{1,0:T(8,128)(2,1)}, bf16[1024,2048]{1,0:T(8,128)(2,1)}) fusion(bf16[1024,2048]{1,0:T(8,128)(2,1)} %all-reduce.10.cloned.1.call-done, bf16[1024,2048]{1,0:T(8,128)(2,1)} %get-tuple-element.84, f32[1024]{0:T(1024)S(1)} %broadcast_multiply_fusion, f32[2048]{0:T(1024)S(1)} %bitcast.271, f32[1024]{0:T(1024)S(1)} %bitcast.273, ...), kind=kLoop, calls=%fused_computation.11 | loop fusion | flops 29360128 | bytes 33570816 | tf_op jit(solution)/shard_map/convert_element_type | solution.py:1036
  1094.1 9.6 all-reduce.4
  1104.9 3.9 slice_bitcast_fusion
  (305 shorter events, 170.4 us)
Async XLA Ops:
  7.2 120.9 %all-gather.3.cloned.1.call-start = ((), (), s32[]{:S(2)}) async-start(), calls=%async_computation.11 | async-start | bytes 8847360 | tf_op jit(solution)/shard_map/all_gather | solution.py:63
  139.2 10.8 copy-start.77
  139.2 11.0 copy-start.56
  150.0 9.9 copy-start
  150.0 9.9 copy-start.2
  150.0 50.1 %collective-permute-start = (bf16[4,4,256,864]{2,3,1,0:T(8,128)(2,1)}, bf16[4,4,256,864]{2,3,1,0:T(8,128)(2,1)}, u32[]{:S(2)}, u32[]{:S(2)}) collective-permute-start(bf16[4,4,256,864]{2,3,1,0:T(8,128)(2,1)} %copy.338), channel_id=1, source_target_pairs={{0,4},{4,0},{8,12},{12,8},{16,20},{20,16},{24,28},{28,24},{1,5},{5... | collective-permute-start | bytes 21233672 | tf_op jit(solution)/shard_map/ppermute | solution.py:55
  150.2 47.7 %copy-start.78 = (f32[4]{0:T(128)}, f32[4]{0:T(128)S(1)}, u32[]{:S(2)}) copy-start(f32[4]{0:T(128)S(1)} %neg.37) | copy-start | bytes 52
  462.7 3.4 copy-start.19
  462.7 4.7 copy-start.20
  469.6 3.9 copy-start.3
  469.6 3.9 copy-start.59
  473.4 141.2 %copy-start.10 = (bf16[4,512,432]{2,1,0:T(8,128)(2,1)}, bf16[4,512,432]{2,1,0:T(8,128)(2,1)S(1)}, u32[]{:S(2)}) copy-start(bf16[4,512,432]{2,1,0:T(8,128)(2,1)S(1)} %get-tuple-element.287) | copy-start | bytes 5308420
  480.0 187.9 %all-to-all-start = ((bf16[8,4,32,432]{3,2,1,0:T(8,128)(2,1)}), bf16[8,4,32,432]{3,2,1,0:T(8,128)(2,1)}, u32[]{:S(2)}, u32[]{:S(2)}) async-start(bf16[8,4,32,432]{3,2,1,0:T(8,128)(2,1)} %copy.353), calls=%async_computation | async-start | bytes 2097152 | tf_op jit(solution)/shard_map/all_to_all | solution.py:108
  484.2 376.4 %all-reduce.8.cloned.1.call-start = ((), (), s32[]{:S(2)}) async-start(), calls=%async_computation.9 | async-start | bytes 8388608 | tf_op jit(solution)/shard_map/psum | solution.py:95
  505.2 11.1 copy-start.81
  505.2 11.1 copy-start.84
  532.5 11.1 copy-start.82
  532.5 11.1 copy-start.83
  560.0 11.3 copy-start.9
  560.0 11.3 copy-start.32
  587.5 9.0 copy-start.13
  587.5 9.0 copy-start.14
  599.7 3.8 copy-start.18
  607.9 6.7 copy-start.58
  607.9 6.7 copy-start.79
  614.4 65.2 %collective-permute-start.1 = (bf16[4,4,256,864]{2,3,1,0:T(8,128)(2,1)}, bf16[4,4,256,864]{2,3,1,0:T(8,128)(2,1)}, u32[]{:S(2)}, u32[]{:S(2)}) collective-permute-start(bf16[4,4,256,864]{2,3,1,0:T(8,128)(2,1)} %pad_maximum_fusion), channel_id=1, source_target_pairs={{0,4},{4,0},{8,12},{12,8},{16,20},{20,16},{24,28},{28,24},{1,5},{5... | collective-permute-start | bytes 21233672 | tf_op jit(solution)/shard_map/ppermute | solution.py:55
  619.5 4.0 copy-start.1
  619.5 4.0 copy-start.23
  657.5 11.9 %copy-start.62 = (f32[4]{0:T(128)S(1)}, f32[4]{0:T(128)}, u32[]{:S(2)}) copy-start(f32[4]{0:T(128)} %get-tuple-element.349) | copy-start | bytes 52
  657.5 11.9 %copy-start.69 = (f32[4]{0:T(128)S(1)}, f32[4]{0:T(128)}, u32[]{:S(2)}) copy-start(f32[4]{0:T(128)} %get-tuple-element.348) | copy-start | bytes 52
  675.3 19.7 %all-to-all-start.1 = ((bf16[8,4,32,432]{3,2,1,0:T(8,128)(2,1)}), bf16[8,4,32,432]{3,2,1,0:T(8,128)(2,1)}, u32[]{:S(2)}, u32[]{:S(2)}) async-start(bf16[8,4,32,432]{3,2,1,0:T(8,128)(2,1)} %broadcast_dynamic-update-slice_fusion), calls=%async_computation.1 | async-start | bytes 2097152 | tf_op jit(solution)/shard_map/all_to_all | solution.py:116
  679.6 257.3 %reduce-scatter.4.cloned.1.call-start = ((), (), s32[]{:S(2)}) async-start(), calls=%async_computation.12 | async-start | bytes 8847360
  689.9 6.5 copy-start.60
  699.4 3.5 copy-start.24
  699.4 3.5 copy-start.53
  710.6 3.6 copy-start.25
  813.0 5.6 copy-start.38
  813.0 5.5 copy-start.39
  815.3 4.6 copy-start.37
  822.5 6.4 copy-start.26
  824.9 28.7 %all-to-all-start.4 = ((bf16[8,1,256,432]{2,3,1,0:T(8,128)(2,1)}), bf16[8,1,256,432]{2,3,1,0:T(8,128)(2,1)S(1)}, u32[]{:S(2)}, u32[]{:S(2)}) async-start(bf16[8,1,256,432]{2,3,1,0:T(8,128)(2,1)} %fusion.29), calls=%async_computation.4 | async-start | bytes 3538944 | tf_op jit(solution)/shard_map/all_to_all | solution.py:158
  828.9 6.8 copy-start.55
  828.9 6.8 copy-start.80
  835.7 5.6 copy-start.29
  835.7 5.6 copy-start.48
  853.6 4.2 copy-start.28
  853.6 50.7 %all-to-all-start.3 = ((f32[8,1,256]{2,1,0:T(1,128)}), f32[8,1,256]{2,1,0:T(1,128)S(1)}, u32[]{:S(2)}, u32[]{:S(2)}) async-start(f32[8,1,256]{2,1,0:T(1,128)} %bitcast.35), calls=%async_computation.3 | async-start | bytes 16384 | tf_op jit(solution)/shard_map/all_to_all | solution.py:100
  857.7 172.3 %all-reduce.10.cloned.1.call-start = ((), (), s32[]{:S(2)}) async-start(), calls=%async_computation.10 | async-start | bytes 8388608 | tf_op jit(solution)/shard_map/psum | solution.py:95
  904.3 7.7 copy-start.57
  904.3 27.5 %all-to-all-start.5 = ((bf16[8,1,256,432]{2,3,1,0:T(8,128)(2,1)}), bf16[8,1,256,432]{2,3,1,0:T(8,128)(2,1)S(1)}, u32[]{:S(2)}, u32[]{:S(2)}) async-start(bf16[8,1,256,432]{2,3,1,0:T(8,128)(2,1)} %copy.385), calls=%async_computation.5 | async-start | bytes 3538944 | tf_op jit(solution)/shard_map/all_to_all | solution.py:162
  913.2 9.8 copy-start.40
  941.9 3.4 copy-start.34
  953.5 84.3 %all-to-all-start.6 = ((bf16[8,1,256,432]{2,3,1,0:T(8,128)(2,1)}), bf16[8,1,256,432]{2,3,1,0:T(8,128)(2,1)S(1)}, u32[]{:S(2)}, u32[]{:S(2)}) async-start(bf16[8,1,256,432]{2,3,1,0:T(8,128)(2,1)} %maximum_bitcast_fusion), calls=%async_computation.6 | async-start | bytes 3538944 | tf_op jit(solution)/shard_map/all_to_all | solution.py:158
  960.7 69.3 %copy-start.61 = (f32[8,1,256]{2,1,0:T(1,128)S(1)}, f32[8,1,256]{2,1,0:T(1,128)}, u32[]{:S(2)}) copy-start(f32[8,1,256]{2,1,0:T(1,128)} %get-tuple-element.339) | copy-start | bytes 24580
  1039.0 37.4 %all-to-all-start.2 = ((f32[8,1,256]{2,1,0:T(1,128)}), f32[8,1,256]{2,1,0:T(1,128)S(1)}, u32[]{:S(2)}, u32[]{:S(2)}) async-start(f32[8,1,256]{2,1,0:T(1,128)} %bitcast.34), calls=%async_computation.2 | async-start | bytes 16384 | tf_op jit(solution)/shard_map/all_to_all | solution.py:100
  1076.3 50.4 %all-to-all-start.7 = ((bf16[8,1,256,432]{2,3,1,0:T(8,128)(2,1)}), bf16[8,1,256,432]{2,3,1,0:T(8,128)(2,1)S(1)}, u32[]{:S(2)}, u32[]{:S(2)}) async-start(bf16[8,1,256,432]{2,3,1,0:T(8,128)(2,1)} %copy.398), calls=%async_computation.7 | async-start | bytes 3538944 | tf_op jit(solution)/shard_map/all_to_all | solution.py:162
  1080.8 22.9 %copy-start.66 = (f32[256]{0:T(256)S(1)}, f32[256]{0:T(256)}, u32[]{:S(2)}) copy-start(f32[256]{0:T(256)} %param.28) | copy-start | bytes 3076
  1080.8 22.9 %copy-start.70 = (f32[256]{0:T(256)S(1)}, f32[256]{0:T(256)}, u32[]{:S(2)}) copy-start(f32[256]{0:T(256)} %param.46) | copy-start | bytes 3076
  1080.8 22.9 %copy-start.71 = (f32[256]{0:T(256)S(1)}, f32[256]{0:T(256)}, u32[]{:S(2)}) copy-start(f32[256]{0:T(256)} %param.47) | copy-start | bytes 3076
  1080.8 23.5 %copy-start.68 = (f32[256]{0:T(256)S(1)}, f32[256]{0:T(256)}, u32[]{:S(2)}) copy-start(f32[256]{0:T(256)} %param.29) | copy-start | bytes 3076
  1080.8 23.5 %copy-start.72 = (f32[256]{0:T(256)S(1)}, f32[256]{0:T(256)}, u32[]{:S(2)}) copy-start(f32[256]{0:T(256)} %param.48) | copy-start | bytes 3076
  1080.8 23.5 %copy-start.73 = (f32[256]{0:T(256)S(1)}, f32[256]{0:T(256)}, u32[]{:S(2)}) copy-start(f32[256]{0:T(256)} %param.49) | copy-start | bytes 3076
  1103.7 5.2 copy-start.74
  1103.7 5.2 copy-start.75
  (35 other events, 79.5 us)
Sparse Core Ops, SparseCore 0:
  12.0 116.0 all-gather.2
  487.4 156.7 all-reduce.7
  690.0 130.9 reduce-scatter.3
  873.4 156.5 all-reduce.9
